TPU v7x, 768 devices: a whole 4x8x12 slice. The times are simulated.
768 devices in a mesh: sfc: 96 (over x, z, core), grp: 8 (over y).
Axes of the slice: x: 4, y: 8, z: 12, core: 2. Of those that a mesh axis runs over, the one named last changes fastest.
Arguments:
- source: float32 [384, 16, 2048], P('sfc', None, 'grp'), may hold values from -8 to 8
- layer_counts: int32 [96], P('sfc'), may hold values from 1 to 4, 256 in all
Outputs:
- solution: float32 [384, 16, 2048], P('sfc', None, 'grp')
- residual: float32 [384, 16, 2048], P('sfc', None, 'grp')
- direction: float32 [384, 16, 2048], P('sfc', None, 'grp')
Inputs may be any that keep to these rules, and one draw needn't show every extreme that they name: `layer_counts`: each entry counts the live leading slots of that index of sfc; they sum to 256, and at least one entry equals 4.
All inputs are finite; a program needn't handle non-finite values. No bound on the sum of `layer_counts` on one device may be relied on, other than what follows from the above.
Results may differ from a plain program's by a relative error of at most 0.00011.
Values sent between devices are 32-bit elements; how exact they have to be, the bound alone decides.
A program may use at most 32 MiB of HBM per device.

v0:
```python
import jax
import jax.numpy as jnp
from jax import lax
from jax.sharding import Mesh
from jax.sharding import PartitionSpec as P

PRE_SWEEPS = 2
POST_SWEEPS = 2
COARSE_SWEEPS = 4
SFC = ("sfc_0", "sfc_1", "sfc_2")
SFC_GRP = ("sfc_0", "sfc_1", "sfc_2", "grp")


OMEGA = 2.0 / 3.0


def padded_2(cells, sides, width):
    for axis, dim in sides:
        count = lax.axis_size(axis)
        ends = count - 1
        head = lax.slice_in_dim(cells, 0, width, axis=dim)
        tail = lax.slice_in_dim(cells, cells.shape[dim] - width, cells.shape[dim], axis=dim)
        cells = jnp.concatenate(
            [
                lax.ppermute(tail, axis, [(i, (i + 1) % count) for i in range(ends)]),
                cells,
                lax.ppermute(head, axis, [((i + 1) % count, i) for i in range(ends)]),
            ],
            axis=dim,
        )
    return cells


def laid_out(parts, dim):
    parts = jnp.moveaxis(parts, 0, dim)
    lengths = parts.shape
    return parts.reshape(*lengths[:dim], lengths[dim] * lengths[dim + 1], *lengths[dim + 2 :])


def from_everyone(value, axis):
    devices = lax.axis_size(axis)
    return lax.all_to_all(
        jnp.broadcast_to(value[None], (devices, *value.shape)), axis, 0, 0, tiled=True
    )


def collect(value, axis, dim):
    return laid_out(from_everyone(value, axis), dim)


def one_axis_at_a_time(value, axes):
    for axis in axes:
        value = lax.psum(value, axis)
    return value


def laplace(field, count, edge, outer_faces, side_faces):
    planes, width = field.shape
    plane = lax.broadcasted_iota(jnp.int32, (planes, 1), 0)
    last_index = count * edge - 1
    last = lax.dynamic_slice_in_dim(field, last_index, 1, 0)
    ends = outer_faces(jnp.concatenate([field[:1], last], axis=0))
    below = jnp.concatenate([ends[:1], field[:-1]], axis=0)
    above = jnp.concatenate([field[1:], jnp.zeros((1, width), jnp.float32)], axis=0)
    above = above + jnp.where(plane == last_index, ends[3:], 0.0)
    south, north = side_faces(
        jnp.concatenate([field[:, :edge], field[:, width - edge :]], axis=1), edge
    )
    north_rows = jnp.concatenate([field[:, edge:], north], axis=1)
    south_rows = jnp.concatenate([south, field[:, : width - edge]], axis=1)
    column = lax.broadcasted_iota(jnp.int32, (1, width), 1) % edge
    pad_col = jnp.zeros((planes, 1), jnp.float32)
    up_z = jnp.where(column != edge - 1, jnp.concatenate([field[:, 1:], pad_col], axis=1), 0.0)
    down_z = jnp.where(column != 0, jnp.concatenate([pad_col, field[:, :-1]], axis=1), 0.0)
    total = 6.0 * field - below - above - north_rows - south_rows - up_z - down_z
    return jnp.where(plane < count * edge, total, 0.0)


def padded_laplace(field, edge):
    planes, width = field.shape
    zero_plane = jnp.zeros((1, width), jnp.float32)
    below = jnp.concatenate([zero_plane, field[:-1]], axis=0)
    above = jnp.concatenate([field[1:], zero_plane], axis=0)
    pad_rows = jnp.zeros((planes, edge), jnp.float32)
    north_rows = jnp.concatenate([field[:, edge:], pad_rows], axis=1)
    south_rows = jnp.concatenate([pad_rows, field[:, : width - edge]], axis=1)
    column = lax.broadcasted_iota(jnp.int32, (1, width), 1) % edge
    pad_col = jnp.zeros((planes, 1), jnp.float32)
    up_z = jnp.where(column != edge - 1, jnp.concatenate([field[:, 1:], pad_col], axis=1), 0.0)
    down_z = jnp.where(column != 0, jnp.concatenate([pad_col, field[:, :-1]], axis=1), 0.0)
    return 6.0 * field - below - above - north_rows - south_rows - up_z - down_z


def deep_extend(stacked, count, edge, depth):
    kinds, planes, width = stacked.shape
    last = lax.dynamic_slice_in_dim(stacked, count * edge - depth, depth, 1)
    ends = jnp.concatenate([stacked[:, :depth], last], axis=1)
    got = padded_2(ends, ((SFC, 1),), depth)
    blank = jnp.zeros((kinds, depth, width), jnp.float32)
    extended = jnp.concatenate([got[:, :depth], stacked, blank], axis=1)
    extended = lax.dynamic_update_slice_in_dim(
        extended, got[:, 3 * depth :], depth + count * edge, 1
    )
    span = depth * edge
    faces = jnp.concatenate([extended[:, :, :span], extended[:, :, width - span :]], axis=2)
    wide = padded_2(faces, (("grp", 2),), span)
    return jnp.concatenate([wide[:, :, :span], extended, wide[:, :, 3 * span :]], axis=2)


def deep_mask(count, edge, depth, planes, width):
    span = depth * edge
    sfc_index = lax.axis_index(SFC)
    grp_index = lax.axis_index("grp")
    sfc_last = lax.axis_size(SFC) - 1
    grp_last = lax.axis_size("grp") - 1
    plane = lax.broadcasted_iota(jnp.int32, (planes + 2 * depth, 1), 0)
    live_end = depth + count * edge
    plane_ok = (plane < depth) & (sfc_index > 0) | (plane >= depth) & (plane < live_end)
    plane_ok = plane_ok | (plane >= live_end) & (plane < live_end + depth) & (sfc_index < sfc_last)
    column = lax.broadcasted_iota(jnp.int32, (1, width + 2 * span), 1)
    column_ok = (column < span) & (grp_index > 0) | (column >= span) & (column < span + width)
    column_ok = column_ok | (column >= span + width) & (grp_index < grp_last)
    return plane_ok & column_ok


def trim_live(padded, count, edge, depth, planes, width):
    span = depth * edge
    inner = padded[depth : depth + planes, span : span + width]
    plane = lax.broadcasted_iota(jnp.int32, (planes, 1), 0)
    return jnp.where(plane < count * edge, inner, 0.0)


def fine_ends(ends):
    return padded_2(ends, ((SFC, 0),), 1)


def fine_sides(faces, edge):
    wide = padded_2(faces, (("grp", 1),), edge)
    return (wide[:, :edge], wide[:, 3 * edge :])


def slab_ends(ends):
    return padded_2(ends, ((SFC, 0),), 1)


def closed_sides(faces, edge):
    blank = jnp.zeros((faces.shape[0], edge), jnp.float32)
    return (blank, blank)


def fine_laplace(field, count, edge):
    return laplace(field, count, edge, fine_ends, fine_sides)


def restrict(field, half):
    planes = field.shape[0]
    blocks = field.reshape(planes // 2, 2, half, 2, half, 2)
    return 0.125 * jnp.sum(blocks, axis=(1, 3, 5)).reshape(planes // 2, half * half)


def prolong(coarse, half):
    planes = coarse.shape[0]
    blocks = coarse.reshape(planes, 1, half, 1, half, 1)
    blocks = jnp.broadcast_to(blocks, (planes, 2, half, 2, half, 2))
    return blocks.reshape(planes * 2, 4 * half * half)


def coarse_solve(coarse_rhs, count, half):
    coarse_step = OMEGA / 1.5
    whole_rhs = collect(coarse_rhs, "grp", 1)
    correction = coarse_step * whole_rhs
    for sweep in range(COARSE_SWEEPS - 1):
        applied = laplace(correction, count, half, slab_ends, closed_sides)
        correction = correction + coarse_step * (whole_rhs - 0.25 * applied)
    offset = lax.axis_index("grp") * (half * half)
    return lax.dynamic_slice_in_dim(correction, offset, half * half, 1)


def vcycle(rhs, count, edge):
    step = OMEGA / 6.0
    half = edge // 2
    planes, width = rhs.shape
    depth = max(PRE_SWEEPS, POST_SWEEPS)
    keeper = deep_mask(count, edge, depth, planes, width)
    padded_rhs = deep_extend(rhs[None], count, edge, depth)[0]
    padded_z = step * padded_rhs
    padded_z = jnp.where(
        keeper, padded_z + step * (padded_rhs - padded_laplace(padded_z, edge)), 0.0
    )
    padded_defect = padded_rhs - padded_laplace(padded_z, edge)
    smooth = trim_live(padded_z, count, edge, depth, planes, width)
    defect = trim_live(padded_defect, count, edge, depth, planes, width)
    correction = coarse_solve(restrict(defect, half), count, half)
    smooth = smooth + prolong(correction, half)
    both = deep_extend(jnp.stack([rhs, smooth]), count, edge, depth)
    padded_rhs = both[0]
    padded_z = both[1]
    for sweep in range(POST_SWEEPS):
        padded_z = jnp.where(
            keeper, padded_z + step * (padded_rhs - padded_laplace(padded_z, edge)), 0.0
        )
    return trim_live(padded_z, count, edge, depth, planes, width)


def shards(source, layer_counts):
    count = layer_counts[0]
    slots, edge, width = source.shape
    planes = slots * edge
    plane = lax.broadcasted_iota(jnp.int32, (planes, 1), 0)
    first_rhs = jnp.where(plane < count * edge, source.reshape(planes, width), 0.0)
    first_z = vcycle(first_rhs, count, edge)
    rz_value = one_axis_at_a_time(jnp.sum(first_rhs * first_z), SFC_GRP)
    image = fine_laplace(first_z, count, edge)
    curv = one_axis_at_a_time(jnp.sum(first_z * image), SFC_GRP)
    alpha = rz_value / curv
    solution = alpha * first_z
    residual = first_rhs - alpha * image
    next_z = vcycle(residual, count, edge)
    cross = one_axis_at_a_time(jnp.sum(next_z * image), SFC_GRP)
    direction = next_z - cross / curv * first_z
    shape = (slots, edge, width)
    return (solution.reshape(shape), residual.reshape(shape), direction.reshape(shape))


def solution(mesh):
    finer = Mesh(
        mesh.devices.reshape(4, 12, 2, mesh.shape["grp"]), ("sfc_0", "sfc_1", "sfc_2", "grp")
    )
    in_specs = (P(SFC, None, "grp"), P(SFC))
    out_specs = (P(SFC, None, "grp"), P(SFC, None, "grp"), P(SFC, None, "grp"))
    return jax.shard_map(
        shards, mesh=finer, in_specs=in_specs, out_specs=out_specs, check_vma=False
    )
```

profile of v0, /device:TPU:1, one launch (start us, length us, event | category | flops | bytes accessed | tf_op | source)
XLA Modules:
  0.0 347.9 jit_solution(6161311427206405119)
XLA Ops:
  2.2 12.4 %collective-permute-start.1 = (f32[1,2,256]{2,1,0:T(2,128)S(1)}, f32[1,2,256]{2,1,0:T(2,128)S(1)}, u32[]{:S(2)}, u32[]{:S(2)}) collective-permute-start(f32[1,2,256]{2,1,0:T(2,128)S(1)} %slice.504), channel_id=1, source_target_pairs={{8,0},{16,8},{24,16},{32,24},{40,32},{48,40},{56,48},{64,56},{72,6... | collective-permute-start | bytes 6152 | tf_op jit(solution)/shard_map/ppermute | solution.py:27
  25.7 5.6 %reshape.239 = f32[32,2,8,2,8,2]{5,4,3,2,1,0:T(8,128)} reshape(f32[64,256]{1,0:T(8,128)S(1)} %fusion.61) | data formatting | bytes 131072 | tf_op jit(solution)/shard_map/reshape | solution.py:157
  38.2 7.1 %all-to-all-done = f32[8,1,2048]{2,1,0:T(1,128)S(1)} async-done(((f32[8,1,2048]{2,1,0:T(1,128)}), f32[8,1,2048]{2,1,0:T(1,128)S(1)}, u32[]{:S(2)}, u32[]{:S(2)}) %all-to-all-start) | async-done | bytes 65568 | tf_op jit(solution)/shard_map/all_to_all | solution.py:42
  47.2 4.4 %collective-permute-start.5 = (f32[1,512]{0,1:T(8,128)S(1)}, f32[1,512]{0,1:T(8,128)S(1)}, u32[]{:S(2)}, u32[]{:S(2)}) collective-permute-start(f32[1,512]{0,1:T(8,128)S(1)} %get-tuple-element.60), channel_id=1, source_target_pairs={{8,0},{16,8},{24,16},{32,24},{40,32},{48,40},{56,48},{64,56},{72,6... | collective-permute-start | bytes 6152 | tf_op jit(solution)/shard_map/ppermute | solution.py:27
  61.2 4.4 %collective-permute-start.6 = (f32[1,512]{0,1:T(8,128)S(1)}, f32[1,512]{0,1:T(8,128)S(1)}, u32[]{:S(2)}, u32[]{:S(2)}) collective-permute-start(f32[1,512]{0,1:T(8,128)S(1)} %get-tuple-element.53), channel_id=1, source_target_pairs={{0,8},{8,16},{16,24},{24,32},{32,40},{40,48},{48,56},{56,64},{64,7... | collective-permute-start | bytes 6152 | tf_op jit(solution)/shard_map/ppermute | solution.py:25
  71.5 4.4 %collective-permute-start.8 = (f32[1,512]{0,1:T(8,128)S(1)}, f32[1,512]{0,1:T(8,128)S(1)}, u32[]{:S(2)}, u32[]{:S(2)}) collective-permute-start(f32[1,512]{0,1:T(8,128)S(1)} %get-tuple-element.45), channel_id=1, source_target_pairs={{0,8},{8,16},{16,24},{24,32},{32,40},{40,48},{48,56},{56,64},{64,7... | collective-permute-start | bytes 6152 | tf_op jit(solution)/shard_map/ppermute | solution.py:25
  81.9 4.0 %reshape.241 = f32[64,256]{1,0:T(8,128)S(1)} reshape(f32[32,2,8,2,8,2]{5,4,3,2,1,0:T(8,128)} %broadcast_in_dim.422) | data formatting | bytes 131072 | tf_op jit(solution)/shard_map/reshape | solution.py:165
  86.1 4.4 %collective-permute-start.10 = (f32[2,2,256]{2,1,0:T(2,128)S(1)}, f32[2,2,256]{2,1,0:T(2,128)S(1)}, u32[]{:S(2)}, u32[]{:S(2)}) collective-permute-start(f32[2,2,256]{2,1,0:T(2,128)S(1)} %get-tuple-element.83), channel_id=1, source_target_pairs={{0,8},{8,16},{16,24},{24,32},{32,40},{40,48},{48,56},{56,64},{64,7... | collective-permute-start | bytes 12296 | tf_op jit(solution)/shard_map/ppermute | solution.py:25
  111.2 4.0 %collective-permute-start.17 = (f32[64,16]{1,0:T(8,128)S(1)}, f32[64,16]{1,0:T(8,128)S(1)}, u32[]{:S(2)}, u32[]{:S(2)}) collective-permute-start(f32[64,16]{1,0:T(8,128)S(1)} %get-tuple-element.141), channel_id=1, source_target_pairs={{0,1},{1,2},{2,3},{3,4},{4,5},{5,6},{6,7},{8,9},{9,10},{10,11},{11... | collective-permute-start | bytes 12296 | tf_op jit(solution)/shard_map/ppermute | solution.py:25
  117.0 28.8 %all-reduce.83 = (f32[]{:T(128)}, f32[]{:T(128)}) all-reduce(f32[]{:T(128)} %get-tuple-element.4, f32[]{:T(128)} %get-tuple-element.3), channel_id=1, replica_groups=mesh['sfc_0'=4,'sfc_1'=12,'sfc_2'=2,'grp'=8] {'sfc_0'}, use_global_device_ids=true, to_apply=%region_2.3 | all-reduce | flops 2 | bytes 16 | tf_op jit(solution)/shard_map/psum | solution.py:53
  145.8 18.1 %all-reduce.81 = (f32[]{:T(128)}, f32[]{:T(128)}) all-reduce(f32[]{:T(128)} %get-tuple-element.9, f32[]{:T(128)} %get-tuple-element.10), channel_id=1, replica_groups=mesh['sfc_0'=4,'sfc_1'=12,'sfc_2'=2,'grp'=8] {'sfc_1'}, use_global_device_ids=true, to_apply=%region_3.4 | all-reduce | flops 2 | bytes 16 | tf_op jit(solution)/shard_map/psum | solution.py:53
  163.9 12.9 %all-reduce.84 = (f32[]{:T(128)}, f32[]{:T(128)}) all-reduce(f32[]{:T(128)} %get-tuple-element.5, f32[]{:T(128)} %get-tuple-element.6), channel_id=1, replica_groups=mesh['sfc_0'=4,'sfc_1'=12,'sfc_2'=2,'grp'=8] {'sfc_2'}, use_global_device_ids=true, to_apply=%region_4.5 | all-reduce | flops 2 | bytes 16 | tf_op jit(solution)/shard_map/psum | solution.py:53
  176.8 13.4 %all-reduce.82 = (f32[]{:T(128)}, f32[]{:T(128)}) all-reduce(f32[]{:T(128)} %get-tuple-element.11, f32[]{:T(128)} %get-tuple-element.12), channel_id=1, replica_groups=mesh['sfc_0'=4,'sfc_1'=12,'sfc_2'=2,'grp'=8] {'grp'}, use_global_device_ids=true, to_apply=%region_5.6 | all-reduce | flops 2 | bytes 16 | tf_op jit(solution)/shard_map/psum | solution.py:53
  191.5 7.6 %collective-permute-start.18 = (f32[1,2,256]{2,1,0:T(2,128)S(1)}, f32[1,2,256]{2,1,0:T(2,128)S(1)}, u32[]{:S(2)}, u32[]{:S(2)}) collective-permute-start(f32[1,2,256]{2,1,0:T(2,128)S(1)} %fusion.83), channel_id=1, source_target_pairs={{0,8},{8,16},{16,24},{24,32},{32,40},{40,48},{48,56},{56,64},{64,7... | collective-permute-start | bytes 6152 | tf_op jit(solution)/shard_map/ppermute | solution.py:25
  212.2 5.6 %reshape.244 = f32[32,2,8,2,8,2]{5,4,3,2,1,0:T(8,128)} reshape(f32[64,256]{1,0:T(8,128)S(1)} %fusion.52) | data formatting | bytes 131072 | tf_op jit(solution)/shard_map/reshape | solution.py:157
  220.7 13.1 %all_to_all.10 = f32[8,1,2048]{2,1,0:T(1,128)S(1)} all-to-all(f32[8,1,2048]{2,1,0:T(1,128)S(1)} %reshape.256), channel_id=1, replica_groups=mesh['sfc_0'=4,'sfc_1'=12,'sfc_2'=2,'grp'=8] {'grp'}, dimensions={0} | all-to-all | bytes 131072 | tf_op jit(solution)/shard_map/all_to_all | solution.py:42
  247.6 4.4 %collective-permute-start.24 = (f32[1,512]{0,1:T(8,128)S(1)}, f32[1,512]{0,1:T(8,128)S(1)}, u32[]{:S(2)}, u32[]{:S(2)}) collective-permute-start(f32[1,512]{0,1:T(8,128)S(1)} %get-tuple-element.29), channel_id=1, source_target_pairs={{0,8},{8,16},{16,24},{24,32},{32,40},{40,48},{48,56},{56,64},{64,7... | collective-permute-start | bytes 6152 | tf_op jit(solution)/shard_map/ppermute | solution.py:25
  257.9 4.4 %collective-permute-start.26 = (f32[1,512]{0,1:T(8,128)S(1)}, f32[1,512]{0,1:T(8,128)S(1)}, u32[]{:S(2)}, u32[]{:S(2)}) collective-permute-start(f32[1,512]{0,1:T(8,128)S(1)} %get-tuple-element.21), channel_id=1, source_target_pairs={{0,8},{8,16},{16,24},{24,32},{32,40},{40,48},{48,56},{56,64},{64,7... | collective-permute-start | bytes 6152 | tf_op jit(solution)/shard_map/ppermute | solution.py:25
  268.3 4.0 %reshape.246 = f32[64,256]{1,0:T(8,128)S(1)} reshape(f32[32,2,8,2,8,2]{5,4,3,2,1,0:T(8,128)} %broadcast_in_dim.436) | data formatting | bytes 131072 | tf_op jit(solution)/shard_map/reshape | solution.py:165
  272.5 4.4 %collective-permute-start.28 = (f32[2,2,256]{2,1,0:T(2,128)S(1)}, f32[2,2,256]{2,1,0:T(2,128)S(1)}, u32[]{:S(2)}, u32[]{:S(2)}) collective-permute-start(f32[2,2,256]{2,1,0:T(2,128)S(1)} %get-tuple-element.81), channel_id=1, source_target_pairs={{0,8},{8,16},{16,24},{24,32},{32,40},{40,48},{48,56},{56,64},{64,7... | collective-permute-start | bytes 12296 | tf_op jit(solution)/shard_map/ppermute | solution.py:25
  290.9 12.0 %psum.92 = f32[]{:T(128)} all-reduce(f32[]{:T(128)} %get-tuple-element.13), channel_id=1, replica_groups=mesh['sfc_0'=4,'sfc_1'=12,'sfc_2'=2,'grp'=8] {'sfc_0'}, use_global_device_ids=true, to_apply=%region_13.14 | all-reduce | flops 1 | bytes 8 | tf_op jit(solution)/shard_map/psum | solution.py:53
  302.9 23.0 %psum.93 = f32[]{:T(128)} all-reduce(f32[]{:T(128)} %psum.92), channel_id=1, replica_groups=mesh['sfc_0'=4,'sfc_1'=12,'sfc_2'=2,'grp'=8] {'sfc_1'}, use_global_device_ids=true, to_apply=%region_14.15 | all-reduce | flops 1 | bytes 8 | tf_op jit(solution)/shard_map/psum | solution.py:53
  325.9 8.6 %psum.94 = f32[]{:T(128)} all-reduce(f32[]{:T(128)} %psum.93), channel_id=1, replica_groups=mesh['sfc_0'=4,'sfc_1'=12,'sfc_2'=2,'grp'=8] {'sfc_2'}, use_global_device_ids=true, to_apply=%region_15.16 | all-reduce | flops 1 | bytes 8 | tf_op jit(solution)/shard_map/psum | solution.py:53
  334.5 11.4 %psum.95 = f32[]{:T(128)} all-reduce(f32[]{:T(128)} %psum.94), channel_id=1, replica_groups=mesh['sfc_0'=4,'sfc_1'=12,'sfc_2'=2,'grp'=8] {'grp'}, use_global_device_ids=true, to_apply=%region_16.17 | all-reduce | flops 1 | bytes 8 | tf_op jit(solution)/shard_map/psum | solution.py:53
  (211 shorter events, 120.5 us)
Async XLA Ops:
  2.2 16.5 %collective-permute-start.1 = (f32[1,2,256]{2,1,0:T(2,128)S(1)}, f32[1,2,256]{2,1,0:T(2,128)S(1)}, u32[]{:S(2)}, u32[]{:S(2)}) collective-permute-start(f32[1,2,256]{2,1,0:T(2,128)S(1)} %slice.504), channel_id=1, source_target_pairs={{8,0},{16,8},{24,16},{32,24},{40,32},{48,40},{56,48},{64,56},{72,6... | collective-permute-start | bytes 6152 | tf_op jit(solution)/shard_map/ppermute | solution.py:27
  34.9 10.5 %all-to-all-start = ((f32[8,1,2048]{2,1,0:T(1,128)}), f32[8,1,2048]{2,1,0:T(1,128)S(1)}, u32[]{:S(2)}, u32[]{:S(2)}) async-start(f32[8,1,2048]{2,1,0:T(1,128)} %reshape.254), calls=%async_computation | async-start | bytes 131072 | tf_op jit(solution)/shard_map/all_to_all | solution.py:42
  47.2 10.1 %collective-permute-start.5 = (f32[1,512]{0,1:T(8,128)S(1)}, f32[1,512]{0,1:T(8,128)S(1)}, u32[]{:S(2)}, u32[]{:S(2)}) collective-permute-start(f32[1,512]{0,1:T(8,128)S(1)} %get-tuple-element.60), channel_id=1, source_target_pairs={{8,0},{16,8},{24,16},{32,24},{40,32},{48,40},{56,48},{64,56},{72,6... | collective-permute-start | bytes 6152 | tf_op jit(solution)/shard_map/ppermute | solution.py:27
  51.6 6.9 %collective-permute-start.4 = (f32[1,512]{0,1:T(8,128)S(1)}, f32[1,512]{0,1:T(8,128)S(1)}, u32[]{:S(2)}, u32[]{:S(2)}) collective-permute-start(f32[1,512]{0,1:T(8,128)S(1)} %get-tuple-element.61), channel_id=1, source_target_pairs={{0,8},{8,16},{16,24},{24,32},{32,40},{40,48},{48,56},{56,64},{64,7... | collective-permute-start | bytes 6152 | tf_op jit(solution)/shard_map/ppermute | solution.py:25
  59.2 8.4 %collective-permute-start.7 = (f32[1,512]{0,1:T(8,128)S(1)}, f32[1,512]{0,1:T(8,128)S(1)}, u32[]{:S(2)}, u32[]{:S(2)}) collective-permute-start(f32[1,512]{0,1:T(8,128)S(1)} %get-tuple-element.52), channel_id=1, source_target_pairs={{8,0},{16,8},{24,16},{32,24},{40,32},{48,40},{56,48},{64,56},{72,6... | collective-permute-start | bytes 6152 | tf_op jit(solution)/shard_map/ppermute | solution.py:27
  61.2 7.7 %collective-permute-start.6 = (f32[1,512]{0,1:T(8,128)S(1)}, f32[1,512]{0,1:T(8,128)S(1)}, u32[]{:S(2)}, u32[]{:S(2)}) collective-permute-start(f32[1,512]{0,1:T(8,128)S(1)} %get-tuple-element.53), channel_id=1, source_target_pairs={{0,8},{8,16},{16,24},{24,32},{32,40},{40,48},{48,56},{56,64},{64,7... | collective-permute-start | bytes 6152 | tf_op jit(solution)/shard_map/ppermute | solution.py:25
  69.6 8.4 %collective-permute-start.9 = (f32[1,512]{0,1:T(8,128)S(1)}, f32[1,512]{0,1:T(8,128)S(1)}, u32[]{:S(2)}, u32[]{:S(2)}) collective-permute-start(f32[1,512]{0,1:T(8,128)S(1)} %get-tuple-element.44), channel_id=1, source_target_pairs={{8,0},{16,8},{24,16},{32,24},{40,32},{48,40},{56,48},{64,56},{72,6... | collective-permute-start | bytes 6152 | tf_op jit(solution)/shard_map/ppermute | solution.py:27
  71.5 7.7 %collective-permute-start.8 = (f32[1,512]{0,1:T(8,128)S(1)}, f32[1,512]{0,1:T(8,128)S(1)}, u32[]{:S(2)}, u32[]{:S(2)}) collective-permute-start(f32[1,512]{0,1:T(8,128)S(1)} %get-tuple-element.45), channel_id=1, source_target_pairs={{0,8},{8,16},{16,24},{24,32},{32,40},{40,48},{48,56},{56,64},{64,7... | collective-permute-start | bytes 6152 | tf_op jit(solution)/shard_map/ppermute | solution.py:25
  86.1 6.3 %collective-permute-start.10 = (f32[2,2,256]{2,1,0:T(2,128)S(1)}, f32[2,2,256]{2,1,0:T(2,128)S(1)}, u32[]{:S(2)}, u32[]{:S(2)}) collective-permute-start(f32[2,2,256]{2,1,0:T(2,128)S(1)} %get-tuple-element.83), channel_id=1, source_target_pairs={{0,8},{8,16},{16,24},{24,32},{32,40},{40,48},{48,56},{56,64},{64,7... | collective-permute-start | bytes 12296 | tf_op jit(solution)/shard_map/ppermute | solution.py:25
  90.5 4.9 %collective-permute-start.11 = (f32[2,2,256]{2,1,0:T(2,128)S(1)}, f32[2,2,256]{2,1,0:T(2,128)S(1)}, u32[]{:S(2)}, u32[]{:S(2)}) collective-permute-start(f32[2,2,256]{2,1,0:T(2,128)S(1)} %get-tuple-element.82), channel_id=1, source_target_pairs={{8,0},{16,8},{24,16},{32,24},{40,32},{48,40},{56,48},{64,56},{72,6... | collective-permute-start | bytes 12296 | tf_op jit(solution)/shard_map/ppermute | solution.py:27
  97.7 5.1 %collective-permute-start.13 = (f32[2,68,32]{2,1,0:T(8,128)S(1)}, f32[2,68,32]{2,1,0:T(8,128)S(1)}, u32[]{:S(2)}, u32[]{:S(2)}) collective-permute-start(f32[2,68,32]{2,1,0:T(8,128)S(1)} %get-tuple-element.79), channel_id=1, source_target_pairs={{1,0},{2,1},{3,2},{4,3},{5,4},{6,5},{7,6},{9,8},{10,9},{11,10},{12... | collective-permute-start | bytes 52232 | tf_op jit(solution)/shard_map/ppermute | solution.py:27
  104.2 11.0 %collective-permute-start.14 = (f32[1,256]{1,0:T(1,128)S(1)}, f32[1,256]{1,0:T(1,128)S(1)}, u32[]{:S(2)}, u32[]{:S(2)}) collective-permute-start(f32[1,256]{1,0:T(1,128)S(1)} %get-tuple-element.134), channel_id=1, source_target_pairs={{0,8},{8,16},{16,24},{24,32},{32,40},{40,48},{48,56},{56,64},{64,7... | collective-permute-start | bytes 3080 | tf_op jit(solution)/shard_map/ppermute | solution.py:25
  108.0 7.3 %collective-permute-start.15 = (f32[1,256]{1,0:T(1,128)S(1)}, f32[1,256]{1,0:T(1,128)S(1)}, u32[]{:S(2)}, u32[]{:S(2)}) collective-permute-start(f32[1,256]{1,0:T(1,128)S(1)} %get-tuple-element.135), channel_id=1, source_target_pairs={{8,0},{16,8},{24,16},{32,24},{40,32},{48,40},{56,48},{64,56},{72,6... | collective-permute-start | bytes 3080 | tf_op jit(solution)/shard_map/ppermute | solution.py:27
  109.9 5.3 %collective-permute-start.16 = (f32[64,16]{1,0:T(8,128)S(1)}, f32[64,16]{1,0:T(8,128)S(1)}, u32[]{:S(2)}, u32[]{:S(2)}) collective-permute-start(f32[64,16]{1,0:T(8,128)S(1)} %get-tuple-element.140), channel_id=1, source_target_pairs={{1,0},{2,1},{3,2},{4,3},{5,4},{6,5},{7,6},{9,8},{10,9},{11,10},{12... | collective-permute-start | bytes 12296 | tf_op jit(solution)/shard_map/ppermute | solution.py:27
  111.2 5.0 %collective-permute-start.17 = (f32[64,16]{1,0:T(8,128)S(1)}, f32[64,16]{1,0:T(8,128)S(1)}, u32[]{:S(2)}, u32[]{:S(2)}) collective-permute-start(f32[64,16]{1,0:T(8,128)S(1)} %get-tuple-element.141), channel_id=1, source_target_pairs={{0,1},{1,2},{2,3},{3,4},{4,5},{5,6},{6,7},{8,9},{9,10},{10,11},{11... | collective-permute-start | bytes 12296 | tf_op jit(solution)/shard_map/ppermute | solution.py:25
  191.5 9.6 %collective-permute-start.18 = (f32[1,2,256]{2,1,0:T(2,128)S(1)}, f32[1,2,256]{2,1,0:T(2,128)S(1)}, u32[]{:S(2)}, u32[]{:S(2)}) collective-permute-start(f32[1,2,256]{2,1,0:T(2,128)S(1)} %fusion.83), channel_id=1, source_target_pairs={{0,8},{8,16},{16,24},{24,32},{32,40},{40,48},{48,56},{56,64},{64,7... | collective-permute-start | bytes 6152 | tf_op jit(solution)/shard_map/ppermute | solution.py:25
  235.2 8.6 %collective-permute-start.23 = (f32[1,512]{0,1:T(8,128)S(1)}, f32[1,512]{0,1:T(8,128)S(1)}, u32[]{:S(2)}, u32[]{:S(2)}) collective-permute-start(f32[1,512]{0,1:T(8,128)S(1)} %get-tuple-element.36), channel_id=1, source_target_pairs={{8,0},{16,8},{24,16},{32,24},{40,32},{48,40},{56,48},{64,56},{72,6... | collective-permute-start | bytes 6152 | tf_op jit(solution)/shard_map/ppermute | solution.py:27
  238.2 6.7 %collective-permute-start.22 = (f32[1,512]{0,1:T(8,128)S(1)}, f32[1,512]{0,1:T(8,128)S(1)}, u32[]{:S(2)}, u32[]{:S(2)}) collective-permute-start(f32[1,512]{0,1:T(8,128)S(1)} %get-tuple-element.37), channel_id=1, source_target_pairs={{0,8},{8,16},{16,24},{24,32},{32,40},{40,48},{48,56},{56,64},{64,7... | collective-permute-start | bytes 6152 | tf_op jit(solution)/shard_map/ppermute | solution.py:25
  245.6 8.4 %collective-permute-start.25 = (f32[1,512]{0,1:T(8,128)S(1)}, f32[1,512]{0,1:T(8,128)S(1)}, u32[]{:S(2)}, u32[]{:S(2)}) collective-permute-start(f32[1,512]{0,1:T(8,128)S(1)} %get-tuple-element.28), channel_id=1, source_target_pairs={{8,0},{16,8},{24,16},{32,24},{40,32},{48,40},{56,48},{64,56},{72,6... | collective-permute-start | bytes 6152 | tf_op jit(solution)/shard_map/ppermute | solution.py:27
  247.6 7.7 %collective-permute-start.24 = (f32[1,512]{0,1:T(8,128)S(1)}, f32[1,512]{0,1:T(8,128)S(1)}, u32[]{:S(2)}, u32[]{:S(2)}) collective-permute-start(f32[1,512]{0,1:T(8,128)S(1)} %get-tuple-element.29), channel_id=1, source_target_pairs={{0,8},{8,16},{16,24},{24,32},{32,40},{40,48},{48,56},{56,64},{64,7... | collective-permute-start | bytes 6152 | tf_op jit(solution)/shard_map/ppermute | solution.py:25
  256.0 8.4 %collective-permute-start.27 = (f32[1,512]{0,1:T(8,128)S(1)}, f32[1,512]{0,1:T(8,128)S(1)}, u32[]{:S(2)}, u32[]{:S(2)}) collective-permute-start(f32[1,512]{0,1:T(8,128)S(1)} %get-tuple-element.20), channel_id=1, source_target_pairs={{8,0},{16,8},{24,16},{32,24},{40,32},{48,40},{56,48},{64,56},{72,6... | collective-permute-start | bytes 6152 | tf_op jit(solution)/shard_map/ppermute | solution.py:27
  257.9 7.7 %collective-permute-start.26 = (f32[1,512]{0,1:T(8,128)S(1)}, f32[1,512]{0,1:T(8,128)S(1)}, u32[]{:S(2)}, u32[]{:S(2)}) collective-permute-start(f32[1,512]{0,1:T(8,128)S(1)} %get-tuple-element.21), channel_id=1, source_target_pairs={{0,8},{8,16},{16,24},{24,32},{32,40},{40,48},{48,56},{56,64},{64,7... | collective-permute-start | bytes 6152 | tf_op jit(solution)/shard_map/ppermute | solution.py:25
  272.5 6.3 %collective-permute-start.28 = (f32[2,2,256]{2,1,0:T(2,128)S(1)}, f32[2,2,256]{2,1,0:T(2,128)S(1)}, u32[]{:S(2)}, u32[]{:S(2)}) collective-permute-start(f32[2,2,256]{2,1,0:T(2,128)S(1)} %get-tuple-element.81), channel_id=1, source_target_pairs={{0,8},{8,16},{16,24},{24,32},{32,40},{40,48},{48,56},{56,64},{64,7... | collective-permute-start | bytes 12296 | tf_op jit(solution)/shard_map/ppermute | solution.py:25
  284.1 5.1 %collective-permute-start.31 = (f32[2,68,32]{2,1,0:T(8,128)S(1)}, f32[2,68,32]{2,1,0:T(8,128)S(1)}, u32[]{:S(2)}, u32[]{:S(2)}) collective-permute-start(f32[2,68,32]{2,1,0:T(8,128)S(1)} %get-tuple-element.77), channel_id=1, source_target_pairs={{1,0},{2,1},{3,2},{4,3},{5,4},{6,5},{7,6},{9,8},{10,9},{11,10},{12... | collective-permute-start | bytes 52232 | tf_op jit(solution)/shard_map/ppermute | solution.py:27
  (11 other events, 153.7 us)
where the time goes:
time: 352 us; the launch traced here: 348 us
  blocking collectives  141 us (40%)
  starting transfers between devices  104 us (30%)
  waiting for transfers between devices  50.1 us (14%)
  local copies, waits for them, and re-layouts  30.7 us (9%)
  other arithmetic  16.8 us (5%)
  between operations  5.14 us (1%)
    psum x8, blocking collectives, one_axis_at_a_time(): value = lax.psum(value, axis)  128 us
    ppermute x16, starting transfers between devices, padded_2(): lax.ppermute(tail, axis, [(i, (i + 1) % count) for i in range(ends)])  58.7 us
    ppermute x16, starting transfers between devices, padded_2(): lax.ppermute(head, axis, [((i + 1) % count, i) for i in range(ends)])  41.8 us
    ppermute x16, waiting for transfers between devices, padded_2(): lax.ppermute(head, axis, [((i + 1) % count, i) for i in range(ends)])  34.8 us
    all_to_all x1, blocking collectives, from_everyone(): lax.all_to_all(jnp.broadcast_to(value[None], (devices, *value.shape)), ax...  13.1 us
    reshape x2, local copies, waits for them, and re-layouts, restrict(): blocks = field.reshape(planes // 2, 2, half, 2, half, 2)  11.1 us
    ppermute x16, waiting for transfers between devices, padded_2(): lax.ppermute(tail, axis, [(i, (i + 1) % count) for i in range(ends)])  8.23 us
    reshape x2, local copies, waits for them, and re-layouts, prolong(): return blocks.reshape(planes * 2, 4 * half * half)  8.07 us
  transfers between devices with their start and end apart: 33, of which 24 were waited for; matrix products, arithmetic and copies ran while one was open for 1% of the time, Pallas kernels for 0%

commit v1 on v0

v1 whole, which is shorter than its diff:
```python
import functools

import jax
import jax.numpy as jnp
from jax import lax
from jax.experimental import pallas as pl
from jax.experimental.pallas import tpu as pltpu
from jax.sharding import PartitionSpec as P

E = 16
OMEGA = 2.0 / 3.0
STEP = OMEGA / 6.0
KEEP = 1.0 - OMEGA
TAU = OMEGA / 1.5
SHAPES = {96: (4, 12, 2), 8: (2, 2, 2)}
MESH = pl.DeviceIdType.MESH
F32 = jnp.float32
ROWS = 48 * E
COARSE = 24 * 8


def others(*axes):
    found = [()]
    for count in axes:
        found = [f + (i,) for f in found for i in range(count)]
    return [f for f in found if any(f)]


def kernel(dims, src_hbm, cnt_ref, z_out, v_out, w_out, tot_out, *scratch):
    nx, nz, nc, ny = dims
    (own, last, ysl, ynl, below, above, r, g, q, t, c1, c2, e, cd, cu, buf_a, buf_b, row,
     load_sem, s1, r1, s2, r2, sa, ra, sb, rb) = scratch
    s = lax.axis_index("sfc")
    y = lax.axis_index("grp")
    ns = nx * nz * nc
    px = s // (nz * nc)
    pz = lax.rem(s // nc, nz)
    pc = lax.rem(s, nc)

    def near(ds, dy):
        return (lax.rem(s + ds + ns, ns), lax.rem(y + dy + ny, ny))

    def line(dz, dc):
        return ((px * nz + lax.rem(pz + dz, nz)) * nc + lax.rem(pc + dc, nc), y)

    def plane(dx, dy):
        return ((lax.rem(px + dx, nx) * nz + pz) * nc + pc, lax.rem(y + dy, ny))

    load = pltpu.make_async_copy(src_hbm, own, load_sem)
    load.start()
    line_set, plane_set = others(nz, nc), others(nx, ny)
    around = [(-1, -1), (-1, 0), (-1, 1), (0, -1), (0, 1), (1, -1), (1, 0), (1, 1)]
    barrier = pltpu.get_barrier_semaphore()
    targets = [near(*o) for o in around] + [line(*o) for o in line_set] + [plane(*o) for o in plane_set]
    for target in targets:
        pl.semaphore_signal(barrier, inc=1, device_id=target, device_id_type=MESH)
    load.wait()
    count = cnt_ref[0]
    last[...] = own[lax.rem(count + 3, 4)]
    pl.semaphore_wait(barrier, len(targets))

    copies = []

    def send(src, dst, k, target, ss, rs):
        copy = pltpu.make_async_remote_copy(
            src_ref=src, dst_ref=dst, send_sem=ss.at[k], recv_sem=rs.at[k],
            device_id=target, device_id_type=MESH)
        copy.start()
        copies.append(copy)

    for j, dy in enumerate((1, 0, -1)):
        send(last, below.at[j], j, near(1, dy), s1, r1)
        send(own.at[0], above.at[j], 3 + j, near(-1, dy), s1, r1)
    send(own, ysl, 6, near(0, 1), s1, r1)
    send(own, ynl, 7, near(0, -1), s1, r1)
    for copy in copies:
        copy.wait_recv()

    zero = jnp.zeros((E, 16 * E), F32)
    pieces = (ysl, own, ynl)
    row_ok = (y > 0, None, y < ny - 1)
    for b in range(3):
        ok = row_ok[b]

        def live(cond, value):
            if ok is not None:
                cond = jnp.logical_and(cond, ok)
            return jnp.where(cond, value, 0.0)

        slots = [live(s > 0, below[b])]
        up = live(s < ns - 1, above[b])
        for k in range(4):
            mine = live(k < count, pieces[b][k])
            slots.append(jnp.where(k == count, up, mine) if k else mine)
        slots.append(jnp.where(count == 4, up, 0.0))
        stack = jnp.concatenate(slots + [zero, zero], axis=0)
        for half in range(2):
            r[pl.ds(b * 256 + half * 128, 128), :] = stack[:, half * 128:half * 128 + 128].T

    lane = lax.broadcasted_iota(jnp.int32, (1, 128), 1)
    end = 16 + 16 * count
    mask = jnp.where((lane < 16) & (s > 0) | (lane >= 16) & (lane < end)
                     | (lane >= end) & (lane < end + 16) & (s < ns - 1), 1.0, 0.0).astype(F32)
    masks = [jnp.where(y > 0, mask, 0.0), mask, jnp.where(y < ny - 1, mask, 0.0)]
    fine_masks = [jnp.broadcast_to(m * STEP, (16, 128)) for m in masks]
    coarse_masks = [jnp.broadcast_to(m * (TAU / 4.0), (8, 128)) for m in masks]
    sub16 = lax.broadcasted_iota(jnp.int32, (16, 128), 0)
    sub8 = lax.broadcasted_iota(jnp.int32, (8, 128), 0)
    even = lax.rem(lax.broadcasted_iota(jnp.int32, (8, 128), 1), 2) == 0

    def total(ref, yy):
        i = 16 * yy
        mid = ref[pl.ds(i, 16), :]
        south, north = ref[pl.ds(i - 16, 16), :], ref[pl.ds(i + 16, 16), :]
        down = jnp.where(sub16 == 0, 0.0, pltpu.roll(mid, 1, 0))
        up = jnp.where(sub16 == 15, 0.0, pltpu.roll(mid, 15, 0))
        left, right = pltpu.roll(mid, 1, 1), pltpu.roll(mid, 127, 1)
        return mid, (south + north) + (down + up) + (left + right)

    def smooth(src, dst, lo, hi, add=None):
        for yy in range(lo, hi):
            mid, six = total(src, yy)
            value = KEEP * mid + fine_masks[yy // 16] * six
            if add is not None:
                value = value + STEP * add[pl.ds(16 * yy, 16), :]
            dst[pl.ds(16 * yy, 16), :] = value

    def restrict(src, c, lo, hi):
        for yc in range(lo, hi):
            i = 32 * yc
            u = (src[pl.ds(i, 8, stride=2), :] + src[pl.ds(i + 1, 8, stride=2), :]
                 + src[pl.ds(i + 16, 8, stride=2), :] + src[pl.ds(i + 17, 8, stride=2), :])
            pair = jnp.where(even, pltpu.roll(u, 127, 1), pltpu.roll(u, 1, 1))
            c[pl.ds(8 * yc, 8), :] = 0.125 * (u + pair)

    def coarse_sweep(c, src, dst, lo, hi):
        for yc in range(lo, hi):
            mid = src[pl.ds(8 * yc, 8), :]
            south, north = src[pl.ds(8 * yc - 8, 8), :], src[pl.ds(8 * yc + 8, 8), :]
            down = jnp.where(sub8 == 0, 0.0, pltpu.roll(mid, 1, 0))
            up = jnp.where(sub8 == 7, 0.0, pltpu.roll(mid, 7, 0))
            left, right = pltpu.roll(mid, 2, 1), pltpu.roll(mid, 126, 1)
            six = (south + north) + (down + up) + (left + right)
            dst[pl.ds(8 * yc, 8), :] = (
                KEEP * mid + TAU * c[pl.ds(8 * yc, 8), :] + coarse_masks[yc // 8] * six)

    def coarse_solve(c, lo, hi):
        e[0, pl.ds(8 * lo, 8 * (hi - lo)), :] = TAU * c[pl.ds(8 * lo, 8 * (hi - lo)), :]
        coarse_sweep(c, e.at[0], e.at[1], lo + 1, hi - 1)
        coarse_sweep(c, e.at[1], e.at[0], lo + 2, hi - 2)
        coarse_sweep(c, e.at[0], e.at[1], lo + 3, hi - 3)

    def corrected(rhs, first, dst, lo, hi):
        for yc in range(lo, hi):
            add = e[1, pl.ds(8 * yc, 8), :]
            for k in range(4):
                at = pl.ds(32 * yc + (k // 2) * 16 + k % 2, 8, stride=2)
                dst[at, :] = STEP * (rhs[at, :] + first[at, :]) + add

    smooth(r, g, 1, 47)
    smooth(g, q, 2, 46)
    restrict(q, c1, 1, 23)
    coarse_solve(c1, 1, 23)
    corrected(r, g, q, 4, 20)
    smooth(q, g, 10, 38, r)
    smooth(g, t, 11, 37, r)
    for yy in range(12, 36):
        mid, six = total(t, yy)
        q[pl.ds(16 * yy, 16), :] = 6.0 * mid - (1.0 / STEP) * fine_masks[yy // 16] * six
    alive = (lane >= 16) & (lane < end)
    v = q
    zv = jnp.zeros((16, 128), F32)
    rz, curv = zv, zv
    for yy in range(16, 32):
        at = pl.ds(16 * yy, 16)
        rz = rz + r[at, :] * t[at, :]
        curv = curv + t[at, :] * v[at, :]

    smooth(v, g, 13, 35)
    smooth(g, r, 14, 34)
    restrict(r, c1, 8, 16)

    mine = c1[pl.ds(64, 64), :]
    moved = pltpu.roll(mine, 112, 1)
    for k in range(2, 5):
        moved = jnp.where(count == k, pltpu.roll(mine, 128 - 16 * k, 1), moved)
    cd[0] = moved
    cu[0] = mine
    copies2 = []

    def send2(src, dst, k, target):
        copy = pltpu.make_async_remote_copy(
            src_ref=src, dst_ref=dst, send_sem=s2.at[k], recv_sem=r2.at[k],
            device_id=target, device_id_type=MESH)
        copy.start()
        copies2.append(copy)

    send2(cd.at[0], cd.at[1], 0, near(1, 0))
    send2(cu.at[0], cu.at[1], 1, near(-1, 0))
    for copy in copies2:
        copy.wait_recv()
    ahead = cu[1]
    moved = pltpu.roll(ahead, 16, 1)
    for k in range(2, 5):
        moved = jnp.where(count == k, pltpu.roll(ahead, 16 * k, 1), moved)
    lo_lane = (lane < 16) & (s > 0)
    hi_lane = (lane >= end) & (lane < end + 16) & (s < ns - 1)
    full = jnp.where(alive, mine, jnp.where(lo_lane, cd[1], jnp.where(hi_lane, moved, 0.0)))
    c2[pl.ds(64, 64), :] = full
    send2(c2.at[pl.ds(64, 32)], c2.at[pl.ds(128, 32)], 2, near(0, -1))
    send2(c2.at[pl.ds(96, 32)], c2.at[pl.ds(32, 32)], 3, near(0, 1))
    for copy in copies2[2:]:
        copy.wait_recv()

    @pl.when(y == 0)
    def _():
        c2[pl.ds(32, 32), :] = jnp.zeros((32, 128), F32)

    @pl.when(y == ny - 1)
    def _():
        c2[pl.ds(128, 32), :] = jnp.zeros((32, 128), F32)

    coarse_solve(c2, 4, 20)
    corrected(v, g, r, 7, 17)
    smooth(r, g, 15, 33, v)
    smooth(g, r, 16, 32, v)
    wv = zv
    for yy in range(16, 32):
        at = pl.ds(16 * yy, 16)
        wv = wv + r[at, :] * v[at, :]

    def dot(acc):
        return jnp.sum(jnp.where(alive, acc, 0.0))

    sums = jnp.where(lane == 0, dot(rz), jnp.where(lane == 1, dot(curv), dot(wv)))

    def all_to_all(value, buf, where, group, ss, rs):
        n = len(group)
        buf[n] = value
        out = []
        for k, o in enumerate(group):
            copy = pltpu.make_async_remote_copy(
                src_ref=buf.at[n], dst_ref=buf.at[k], send_sem=ss.at[k], recv_sem=rs.at[k],
                device_id=where(*o), device_id_type=MESH)
            copy.start()
            out.append(copy)
        return out

    first = all_to_all(sums, buf_a, line, line_set, sa, ra)

    for src, dst in ((t, z_out), (v, v_out), (r, w_out)):
        halves = []
        for half in range(2):
            x = src[pl.ds(256 + half * 128, 128), :]
            halves.append(jnp.where(alive, x, 0.0).T)
        for k in range(4):
            for half in range(2):
                dst[k, :, pl.ds(half * 128, 128)] = halves[half][16 + 16 * k:32 + 16 * k, :]

    for copy in first:
        copy.wait_recv()
    second = all_to_all(jnp.sum(buf_a[...], axis=0), buf_b, plane, plane_set, sb, rb)
    for copy in second:
        copy.wait_recv()
    tot_out[...] = jnp.sum(buf_b[...], axis=0)
    for copy in copies + copies2 + first + second:
        copy.wait_send()


def solution(mesh):
    ns, ny = mesh.shape["sfc"], mesh.shape["grp"]
    nx, nz, nc = SHAPES[ns]
    n_line, n_plane = nz * nc - 1, nx * ny - 1
    dma = pltpu.SemaphoreType.DMA

    def shards(source, layer_counts):
        block = jax.ShapeDtypeStruct((4, E, 16 * E), F32)
        vmem = pl.BlockSpec(memory_space=pltpu.VMEM)
        z0, image, w, total = pl.pallas_call(
            functools.partial(kernel, (nx, nz, nc, ny)),
            out_shape=(block, block, block, jax.ShapeDtypeStruct((1, 128), F32)),
            in_specs=[pl.BlockSpec(memory_space=pl.ANY), pl.BlockSpec(memory_space=pltpu.SMEM)],
            out_specs=(vmem, vmem, vmem, vmem),
            scratch_shapes=[
                pltpu.VMEM((4, E, 256), F32), pltpu.VMEM((E, 256), F32),
                pltpu.VMEM((4, E, 256), F32), pltpu.VMEM((4, E, 256), F32),
                pltpu.VMEM((3, E, 256), F32), pltpu.VMEM((3, E, 256), F32),
                pltpu.VMEM((ROWS, 128), F32), pltpu.VMEM((ROWS, 128), F32),
                pltpu.VMEM((ROWS, 128), F32), pltpu.VMEM((ROWS, 128), F32),
                pltpu.VMEM((COARSE, 128), F32), pltpu.VMEM((COARSE, 128), F32), pltpu.VMEM((2, COARSE, 128), F32),
                pltpu.VMEM((2, 64, 128), F32), pltpu.VMEM((2, 64, 128), F32),
                pltpu.VMEM((n_line + 1, 1, 128), F32), pltpu.VMEM((n_plane + 1, 1, 128), F32),
                pltpu.VMEM((1, 128), F32),
                dma, dma((8,)), dma((8,)), dma((4,)), dma((4,)),
                dma((n_line,)), dma((n_line,)), dma((n_plane,)), dma((n_plane,)),
            ],
            compiler_params=pltpu.CompilerParams(collective_id=0, has_side_effects=True),
        )(source, layer_counts)
        rz, curv, wv = total[0, 0], total[0, 1], total[0, 2]
        alpha = rz / curv
        k = lax.broadcasted_iota(jnp.int32, (4, 1, 1), 0)
        rhs = jnp.where(k < layer_counts[0], source, 0.0)
        return alpha * z0, rhs - alpha * image, alpha * ((wv / curv) * z0 - w)

    spec = P("sfc", None, "grp")
    return jax.shard_map(
        shards, mesh=mesh, in_specs=(spec, P("sfc")), out_specs=(spec, spec, spec), check_vma=False)
```

time: 352 us -> 53.2 us (0.15); the launches traced: 348 us -> 52.9 us
  blocking collectives: 141 us -> 0 us
  starting transfers between devices: 104 us -> 0 us
  waiting for transfers between devices: 50.1 us -> 0 us
  Pallas kernels: 0 us -> 46 us
  local copies, waits for them, and re-layouts: 30.7 us -> 1.21 us
  other arithmetic: 16.8 us -> 1.62 us
    psum x8 -> x0, blocking collectives: 128 us -> none  [one_axis_at_a_time(): value = lax.psum(value, axis)]
    ppermute x32 -> x0, starting transfers between devices: 101 us -> none  [the longest x16 58.7 us: padded_2(): lax.ppermute(tail, axis, [(i, (i + 1) % count) for i in range(ends)])]
    pallas_call x0 -> x1, Pallas kernels: none -> 46 us  [shards(): pl.pallas_call(functools.partial(kernel, (nx, nz, nc, ny)), out_shape=(bl...]
    ppermute x32 -> x0, waiting for transfers between devices: 43 us -> none  [the longest x16 34.8 us: padded_2(): lax.ppermute(head, axis, [((i + 1) % count, i) for i in range(ends)])]
    reshape x4 -> x0, local copies, waits for them, and re-layouts: 19.2 us -> none  [the longest x2 11.1 us: restrict(): blocks = field.reshape(planes // 2, 2, half, 2, half, 2)]
    all_to_all x1 -> x0, blocking collectives: 13.1 us -> none  [from_everyone(): lax.all_to_all(jnp.broadcast_to(value[None], (devices, *value.shape)), ax...]
    all_to_all x1 -> x0, waiting for transfers between devices: 7.11 us -> none  [from_everyone(): lax.all_to_all(jnp.broadcast_to(value[None], (devices, *value.shape)), ax...]
    reduce_sum x4 -> x0, other arithmetic: 6.74 us -> none  [the longest x2 5.2 us: restrict(): jnp.sum(blocks, axis=(1, 3, 5)).reshape(planes // 2, half * half)]
  transfers between devices with their start and end apart: 33 -> 0, of which waited for: 24 -> 0; matrix products, arithmetic and copies ran while one was open for 1% -> 0% of each run, Pallas kernels for 0% -> 0%
where the time goes in v1:
time: 53.2 us; the launch traced here: 52.9 us
  Pallas kernels  46 us (86%)
  between operations  4.02 us (8%)
  other arithmetic  1.62 us (3%)
  local copies, waits for them, and re-layouts  1.21 us (2%)
    pallas_call x1, Pallas kernels, shards(): pl.pallas_call(functools.partial(kernel, (nx, nz, nc, ny)), out_shape=(bl...  46 us
    mul x1, other arithmetic, shards(): return (alpha * z0, rhs - alpha * image, alpha * (wv / curv * z0 - w))  1.61 us

profile of v1, /device:TPU:1, one launch (start us, length us, event | category | flops | bytes accessed | tf_op | source)
XLA Modules:
  0.0 52.9 jit_solution(6134893835092061642)
XLA Ops:
  0.6 0.0 copy-start
  1.3 46.0 %shard_map.49 = (f32[4,16,256]{2,1,0:T(8,128)}, f32[4,16,256]{2,1,0:T(8,128)}, f32[4,16,256]{2,1,0:T(8,128)}, f32[1,128]{1,0:T(1,128)}) custom-call(f32[4,16,256]{2,1,0:T(8,128)} %src_hbm.1, s32[1]{0:T(128)} %copy.5.cnt_ref), custom_call_target="tpu_custom_call" | custom-call | tf_op jit(solution)/shard_map/pallas_call | solution.py:279
  47.4 0.0 copy-start.1
  47.4 0.6 %copy-done.1 = f32[1,128]{1,0:T(1,128)S(1)} copy-done((f32[1,128]{1,0:T(1,128)S(1)}, f32[1,128]{1,0:T(1,128)}, u32[]{:S(2)}) %copy-start.1) | copy-done | bytes 536
  48.0 0.6 %fusion = (f32[1,1]{1,0:T(1,128)}, f32[1,1]{1,0:T(1,128)}, f32[1,1]{1,0:T(1,128)}) fusion(f32[1,128]{1,0:T(1,128)S(1)} %copy-done.1), kind=kLoop, calls=%fused_computation.4 | loop fusion | bytes 24 | tf_op jit(solution)/shard_map/slice | solution.py:299
  51.2 0.0 copy-done
  51.3 1.6 %subtract_multiply_fusion = (f32[4,16,256]{2,1,0:T(8,128)}, f32[4,16,256]{2,1,0:T(8,128)}, f32[4,16,256]{2,1,0:T(8,128)}) fusion(f32[4,16,256]{2,1,0:T(8,128)} %get-tuple-element.10, f32[4,16,256]{2,1,0:T(8,128)} %get-tuple-element.8, f32[]{:T(128)} %bitcast.2, f32[]{:T(128)} %bitcast, f32[4,16,256]{2,1,0:T(8,128)} %get-tuple-element.9, ...), kind=kLoop, calls=%fused_computation | loop fusion | flops 114688 | bytes 458764 | tf_op jit(solution)/shard_map/mul | solution.py:303
  (1 shorter events, 0.0 us)
Async XLA Ops:
  0.6 50.6 %copy-start = (f32[4,16,256]{2,1,0:T(8,128)S(1)}, f32[4,16,256]{2,1,0:T(8,128)}, u32[]{:S(2)}) copy-start(f32[4,16,256]{2,1,0:T(8,128)} %src_hbm.1) | copy-start | bytes 196612
  47.4 0.6 %copy-start.1 = (f32[1,128]{1,0:T(1,128)S(1)}, f32[1,128]{1,0:T(1,128)}, u32[]{:S(2)}) copy-start(f32[1,128]{1,0:T(1,128)} %get-tuple-element.7) | copy-start | bytes 1540

commit v2 on v1

v2 whole, which is shorter than its diff:
```python
import functools

import jax
import jax.numpy as jnp
from jax import lax
from jax.experimental import pallas as pl
from jax.experimental.pallas import tpu as pltpu
from jax.sharding import PartitionSpec as P

E = 16
OMEGA = 2.0 / 3.0
STEP = OMEGA / 6.0
KEEP = 1.0 - OMEGA
TAU = OMEGA / 1.5
QUARTER = TAU / 4.0
SHAPES = {96: (4, 12, 2), 8: (2, 2, 2)}
MESH = pl.DeviceIdType.MESH
F32 = jnp.float32
ROWS = 48 * E
COARSE = 24 * 8
NEED = dict(g=(1, 47), q=(2, 46), c=(1, 23), e1=(2, 22), e2=(3, 21), e3=(4, 20), zp=(8, 40),
            z1=(10, 38), z0=(11, 37), v=(12, 36), g2=(13, 35), q2=(14, 34), c2=(7, 17))


def others(*axes):
    found = [()]
    for count in axes:
        found = [f + (i,) for f in found for i in range(count)]
    return [f for f in found if any(f)]


def kernel(dims, src_hbm, cnt_hbm, sol_ref, res_ref, dir_ref, *scratch):
    nx, nz, nc, ny = dims
    (own, cnt, last, ysl, ynl, below, above, r, g, q, zp, z1, z0, v, g2, q2, w1, w,
     c, e1, e2, e3, c2, kap, cw, cd, cu, zt, vt, wt,
     msg, face, faces, hb, hs, hx, hall, hrow, tot,
     load_sem, s1, r1, s2, r2, sm, rb, rs, rx, sh, rh, st, rt) = scratch
    s = lax.axis_index("sfc")
    y = lax.axis_index("grp")
    ns, size = nx * nz * nc, nz * nc
    px, place = s // size, lax.rem(s, size)
    is_head = place == 1
    plane_set = others(nx, ny)

    load = pltpu.make_async_copy(src_hbm, own, load_sem.at[0])
    load.start()
    load_count = pltpu.make_async_copy(cnt_hbm, cnt, load_sem.at[1])
    load_count.start()

    around = [(1, 1), (1, -1), (-1, 1), (-1, -1), (1, 0), (-1, 0), (0, 1), (0, -1)]
    d_ok = {1: s < ns - 1, -1: s > 0, 0: None}
    y_ok = {1: y < ny - 1, -1: y > 0, 0: None}

    def there(ds, dy):
        conds = [k for k in (d_ok[ds], y_ok[dy]) if k is not None]
        return functools.reduce(jnp.logical_and, conds)

    def near(ds, dy):
        return (s + ds, y + dy)

    def head_of(x, yy):
        return (x * size + 1, yy)

    def plane(dx, dy):
        return (lax.rem(px + dx, nx) * size + 1, lax.rem(y + dy, ny))

    barrier = pltpu.get_barrier_semaphore()

    def greet(target):
        pl.semaphore_signal(barrier, inc=1, device_id=target, device_id_type=MESH)

    for o in around:
        pl.when(there(*o))(functools.partial(greet, near(*o)))

    @pl.when(is_head)
    def _():
        for o in plane_set:
            greet(plane(*o))
        for k in range(size):
            if k != 1:
                greet((px * size + k, y))

        @pl.when(y < ny - 1)
        def _():
            for k in range(size):
                greet((px * size + k, y + 1))

        @pl.when(px < nx - 1)
        def _():
            greet(((px + 1) * size, y))

    one = lambda cond: jnp.where(cond, 1, 0)
    beside = (1 + one(s > 0) + one(s < ns - 1)) * (1 + one(y > 0) + one(y < ny - 1)) - 1
    heads = one(y > 0) + one((place == 0) & (px > 0)) + jnp.where(is_head, len(plane_set), 1)

    load.wait()
    load_count.wait()
    count = cnt[0]
    last[...] = own[lax.rem(count + 3, 4)]
    pl.semaphore_wait(barrier, beside + heads)

    def copy_to(src, dst, ss, rs_, target):
        return pltpu.make_async_remote_copy(
            src_ref=src, dst_ref=dst, send_sem=ss, recv_sem=rs_, device_id=target, device_id_type=MESH)

    halo = {}
    for k, (ds, dy) in enumerate(around):
        if ds == 0:
            continue
        src, box = (last, below) if ds == 1 else (own.at[0], above)
        halo[ds, dy] = [copy_to(src, box.at[1 - dy], s1.at[k], r1.at[k], near(ds, dy))]
    for k, (dy, box) in enumerate(((1, ysl), (-1, ynl))):
        halo[0, dy] = []
        for part in range(2):
            half = pl.ds(128 * (1 - part if dy == 1 else part), 128)
            i = 6 + 2 * k + part
            halo[0, dy].append(copy_to(own.at[:, :, half], box.at[:, :, half], s1.at[i], r1.at[i], near(0, dy)))
    for part in range(2):
        for o in around:
            if part < len(halo[o]):
                pl.when(there(*o))(halo[o][part].start)

    def arrived(ds, dy, part=0):
        pl.when(there(-ds, -dy))(halo[ds, dy][part].wait_recv)

    pieces = (ysl, own, ynl)
    row_ok = (y > 0, None, y < ny - 1)

    def assemble(b, half):
        at = pl.ds(128 * half, 128)
        ok = row_ok[b]

        def live(cond, value):
            if ok is not None:
                cond = jnp.logical_and(cond, ok)
            return jnp.where(cond, value, 0.0)

        slots = [live(s > 0, below[b, :, at])]
        up = live(s < ns - 1, above[b, :, at])
        for k in range(4):
            mine = live(k < count, pieces[b][k, :, at])
            slots.append(jnp.where(k == count, up, mine) if k else mine)
        slots.append(jnp.where(count == 4, up, 0.0))
        zero = jnp.zeros((2 * E, 128), F32)
        r[pl.ds(b * 256 + half * 128, 128), :] = jnp.concatenate(slots + [zero], axis=0).T

    lane = lax.broadcasted_iota(jnp.int32, (1, 128), 1)
    end = 16 + 16 * count
    mask = jnp.where((lane < 16) & (s > 0) | (lane >= 16) & (lane < end)
                     | (lane >= end) & (lane < end + 16) & (s < ns - 1), 1.0, 0.0).astype(F32)
    masks = [jnp.where(y > 0, mask, 0.0), mask, jnp.where(y < ny - 1, mask, 0.0)]
    fine_masks = [jnp.broadcast_to(m * STEP, (16, 128)) for m in masks]
    coarse_masks = [jnp.broadcast_to(m * QUARTER, (8, 128)) for m in masks]
    sub16 = lax.broadcasted_iota(jnp.int32, (16, 128), 0)
    sub8 = lax.broadcasted_iota(jnp.int32, (8, 128), 0)
    even = lax.rem(lax.broadcasted_iota(jnp.int32, (8, 128), 1), 2) == 0
    alive = (lane >= 16) & (lane < end)

    def total(ref, yy):
        i = 16 * yy
        mid = ref[pl.ds(i, 16), :]
        south, north = ref[pl.ds(i - 16, 16), :], ref[pl.ds(i + 16, 16), :]
        down = jnp.where(sub16 == 0, 0.0, pltpu.roll(mid, 1, 0))
        up = jnp.where(sub16 == 15, 0.0, pltpu.roll(mid, 15, 0))
        left, right = pltpu.roll(mid, 1, 1), pltpu.roll(mid, 127, 1)
        return mid, (south + north) + (down + up) + (left + right)

    def coarse_total(ref, yc):
        mid = ref[pl.ds(8 * yc, 8), :]
        south, north = ref[pl.ds(8 * yc - 8, 8), :], ref[pl.ds(8 * yc + 8, 8), :]
        down = jnp.where(sub8 == 0, 0.0, pltpu.roll(mid, 1, 0))
        up = jnp.where(sub8 == 7, 0.0, pltpu.roll(mid, 7, 0))
        left, right = pltpu.roll(mid, 2, 1), pltpu.roll(mid, 126, 1)
        return mid, (south + north) + (down + up) + (left + right)

    def smooth(src, dst, add=None):
        def row(yy):
            mid, six = total(src, yy)
            value = KEEP * mid + fine_masks[yy // 16] * six
            if add is not None:
                value = value + STEP * add[pl.ds(16 * yy, 16), :]
            dst[pl.ds(16 * yy, 16), :] = value
        return row

    def apply(src, dst):
        def row(yy):
            mid, six = total(src, yy)
            dst[pl.ds(16 * yy, 16), :] = 6.0 * mid - (1.0 / STEP) * fine_masks[yy // 16] * six
        return row

    def restrict(src, dst):
        def row(yc):
            i = 32 * yc
            u = (src[pl.ds(i, 8, stride=2), :] + src[pl.ds(i + 1, 8, stride=2), :]
                 + src[pl.ds(i + 16, 8, stride=2), :] + src[pl.ds(i + 17, 8, stride=2), :])
            pair = jnp.where(even, pltpu.roll(u, 127, 1), pltpu.roll(u, 1, 1))
            dst[pl.ds(8 * yc, 8), :] = 0.125 * (u + pair)
        return row

    def coarse_first(rhs, dst):
        def row(yc):
            mid, six = coarse_total(rhs, yc)
            dst[pl.ds(8 * yc, 8), :] = (TAU * (1.0 + KEEP)) * mid + TAU * (coarse_masks[yc // 8] * six)
        return row

    def coarse_sweep(rhs, src, dst):
        def row(yc):
            mid, six = coarse_total(src, yc)
            dst[pl.ds(8 * yc, 8), :] = (
                KEEP * mid + TAU * rhs[pl.ds(8 * yc, 8), :] + coarse_masks[yc // 8] * six)
        return row

    def corrected(rhs, first, coarse, dst):
        def pair(yc):
            add = coarse[pl.ds(8 * yc, 8), :]
            for k in range(4):
                at = pl.ds(32 * yc + (k // 2) * 16 + k % 2, 8, stride=2)
                dst[at, :] = STEP * (rhs[at, :] + first[at, :]) + add
        return pair

    def rows(fn, lo, hi):
        for i in range(lo, hi):
            fn(i)

    shrink = lambda lo, hi: (lo + 1, hi - 1)
    halve = lambda lo, hi: (-(-lo // 2), hi // 2)
    double = lambda lo, hi: (2 * lo, 2 * hi)
    stages = [
        ("g", "r", shrink, smooth(r, g)), ("q", "g", shrink, smooth(g, q)),
        ("c", "q", halve, restrict(q, c)), ("e1", "c", shrink, coarse_first(c, e1)),
        ("e2", "e1", shrink, coarse_sweep(c, e1, e2)), ("e3", "e2", shrink, coarse_sweep(c, e2, e3)),
        ("zp", "e3", double, corrected(r, g, e3, zp)), ("z1", "zp", shrink, smooth(zp, z1, r)),
        ("z0", "z1", shrink, smooth(z1, z0, r)), ("v", "z0", shrink, apply(z0, v)),
        ("g2", "v", shrink, smooth(v, g2)), ("q2", "g2", shrink, smooth(g2, q2)),
        ("c2", "q2", halve, restrict(q2, c2)),
    ]
    done = {}

    def advance(lo, hi):
        have = {"r": (lo, hi)}
        for name, source, change, fn in stages:
            new_lo, new_hi = change(*have[source])
            new_lo, new_hi = max(new_lo, NEED[name][0]), min(new_hi, NEED[name][1])
            if new_lo >= new_hi:
                break
            have[name] = (new_lo, new_hi)
            old = done.get(name)
            spans = [(new_lo, new_hi)] if old is None else [(new_lo, old[0]), (old[1], new_hi)]
            for span in spans:
                if name == "zp":
                    rows(fn, span[0] // 2, span[1] // 2)
                else:
                    rows(fn, *span)
            done[name] = (new_lo, new_hi)

    arrived(1, 0)
    arrived(-1, 0)
    assemble(1, 0)
    assemble(1, 1)
    advance(16, 32)
    for dy, b, half in ((1, 0, 1), (-1, 2, 0)):
        arrived(1, dy)
        arrived(-1, dy)
        arrived(0, dy, 0)
        assemble(b, half)
    advance(8, 40)
    for dy, b, half in ((1, 0, 0), (-1, 2, 1)):
        arrived(0, dy, 1)
        assemble(b, half)
    advance(0, 48)

    def keep_alive(value):
        return jnp.where(alive, value, 0.0)

    rz = jnp.zeros((16, 128), F32)
    curv, fine = rz, rz
    for yy in range(16, 32):
        at = pl.ds(16 * yy, 16)
        vy, gy, qy, zy = v[at, :], g2[at, :], q2[at, :], z0[at, :]
        rz = rz + r[at, :] * zy
        curv = curv + zy * vy
        fine = fine + (vy * (vy + gy + qy) + gy * qy)
    for yc in range(8, 16):
        mid, six = coarse_total(c2, yc)
        kap[pl.ds(8 * (yc - 7), 8), :] = keep_alive(KEEP * mid + coarse_masks[1] * six)
    blank = jnp.zeros((8, 128), F32)
    kap[pl.ds(0, 8), :] = blank
    kap[pl.ds(72, 8), :] = blank
    coarse = blank
    for yc in range(8, 16):
        k, six = coarse_total(kap, yc - 7)
        cc = c2[pl.ds(8 * yc, 8), :]
        coarse = coarse + (cc * (cc + k) + k * ((1.0 + KEEP) * k + QUARTER * six))
    column = lambda value: jnp.sum(keep_alive(value), axis=0, keepdims=True)
    inner = kap[pl.ds(8, 64), :]
    turned = jnp.concatenate([inner, inner], axis=0).T
    first_plane, last_plane = turned[16:17], turned[31:32]
    for k in range(2, 5):
        last_plane = jnp.where(count == k, turned[15 + 16 * k:16 + 16 * k], last_plane)
    d_face = jnp.where(lane < 64, first_plane, last_plane)
    even4 = even[:4]
    packed = lambda f: jnp.where(even4, f[:4], f[4:])
    north_face, south_face = packed(kap[pl.ds(64, 8), :]), packed(kap[pl.ds(8, 8), :])
    msg[...] = jnp.concatenate(
        [column(rz), column(curv), STEP * column(fine) + (4.0 * TAU) * column(coarse), d_face, north_face], axis=0)
    face[...] = south_face
    faces[...] = d_face
    to_head = copy_to(msg, hb.at[pl.ds(pl.multiple_of(8 * place, 8), 8)], sm.at[0], rb.at[place], head_of(px, y))
    to_south = copy_to(face, hs.at[pl.ds(pl.multiple_of(4 * place, 4), 4)], sm.at[1], rs.at[place], head_of(px, y - 1))
    to_back = copy_to(faces, hx, sm.at[2], rx, head_of(px - 1, y))
    pl.when(jnp.logical_not(is_head))(to_head.start)
    pl.when(y > 0)(to_south.start)
    pl.when((place == 0) & (px > 0))(to_back.start)

    mine = c2[pl.ds(64, 64), :]

    def shifted(value, sign):
        out = pltpu.roll(value, (16 * sign) % 128, 1)
        for k in range(2, 5):
            out = jnp.where(count == k, pltpu.roll(value, (16 * k * sign) % 128, 1), out)
        return out

    cd[0] = shifted(mine, -1)
    cu[0] = mine
    along = [copy_to(cd.at[0], cd.at[1], s2.at[0], r2.at[0], near(1, 0)),
             copy_to(cu.at[0], cu.at[1], s2.at[1], r2.at[1], near(-1, 0))]
    pl.when(s < ns - 1)(along[0].start)
    pl.when(s > 0)(along[1].start)

    def turn_back(src, dst):
        for half in range(2):
            x = keep_alive(src[pl.ds(256 + half * 128, 128), :]).T
            for k in range(4):
                dst[k, :, pl.ds(half * 128, 128)] = x[16 + 16 * k:32 + 16 * k, :]

    pl.when(s > 0)(along[0].wait_recv)
    pl.when(s < ns - 1)(along[1].wait_recv)
    lo_lane = (lane < 16) & (s > 0)
    hi_lane = (lane >= end) & (lane < end + 16) & (s < ns - 1)
    cw[pl.ds(64, 64), :] = jnp.where(
        alive, mine, jnp.where(lo_lane, cd[1], jnp.where(hi_lane, shifted(cu[1], 1), 0.0)))
    across = [copy_to(cw.at[pl.ds(64, 32)], cw.at[pl.ds(128, 32)], s2.at[2], r2.at[2], near(0, -1)),
              copy_to(cw.at[pl.ds(96, 32)], cw.at[pl.ds(32, 32)], s2.at[3], r2.at[3], near(0, 1))]
    pl.when(y > 0)(across[0].start)
    pl.when(y < ny - 1)(across[1].start)

    def member(k):
        return copy_to(msg, hb.at[pl.ds(8 * k, 8)], sm.at[0], rb.at[k], head_of(px, y))

    def beyond(k):
        return copy_to(face, hs.at[pl.ds(4 * k, 4)], sm.at[1], rs.at[k], head_of(px, y))

    def round_of(k):
        return copy_to(hall.at[len(plane_set)], hall.at[k], sh.at[k], rh.at[k], plane(*plane_set[k]))

    @pl.when(is_head)
    def _():
        hb[pl.ds(8, 8), :] = msg[...]
        for k in range(size):
            if k != 1:
                member(k).wait_recv()

        @pl.when(y < ny - 1)
        def _():
            for k in range(size):
                beyond(k).wait_recv()

        pl.when(px < nx - 1)(to_back.wait_recv)
        acc = hb[pl.ds(0, 8), :]
        for k in range(1, size):
            acc = acc + hb[pl.ds(8 * k, 8), :]
        sides = jnp.zeros((4, 128), F32)
        for k in range(size):
            sides = sides + hb[pl.ds(8 * k + 4, 4), :] * hs[pl.ds(4 * k, 4), :]
        sides = jnp.where(y < ny - 1, sides, 0.0)
        front = hb[pl.ds(3, size, stride=8), :]
        ends = pltpu.roll(front, 64, 1)
        chain = jnp.sum(ends[:size - 1] * hb[pl.ds(11, size - 1, stride=8), :], axis=0, keepdims=True)
        chain = chain + jnp.where(px < nx - 1, ends[size - 1:] * hx[...], 0.0)
        cross = jnp.where(lane < 64, chain, 0.0) + jnp.sum(sides, axis=0, keepdims=True)
        three = jnp.concatenate([acc[:2], acc[2:3] + (16.0 * TAU * QUARTER) * cross], axis=0)
        sums = jnp.sum(three, axis=1, keepdims=True)
        hall[len(plane_set)] = jnp.where(lane == 0, sums[:1], jnp.where(lane == 1, sums[1:2], sums[2:]))
        for k in range(len(plane_set)):
            round_of(k).start()

    turn_back(z0, zt)
    turn_back(v, vt)

    pl.when(y > 0)(across[1].wait_recv)
    pl.when(y < ny - 1)(across[0].wait_recv)
    outside = jnp.zeros((32, 128), F32)

    @pl.when(y == 0)
    def _():
        cw[pl.ds(32, 32), :] = outside

    @pl.when(y == ny - 1)
    def _():
        cw[pl.ds(128, 32), :] = outside

    rows(coarse_first(cw, e1), 5, 19)
    rows(coarse_sweep(cw, e1, e2), 6, 18)
    rows(coarse_sweep(cw, e2, e3), 7, 17)
    rows(corrected(v, g2, e3, zp), 7, 17)
    rows(smooth(zp, w1, v), 15, 33)
    rows(smooth(w1, w, v), 16, 32)
    turn_back(w, wt)

    def news(k):
        return copy_to(hrow, tot, st.at[k], rt, (px * size + k, y))

    @pl.when(is_head)
    def _():
        for k in range(len(plane_set)):
            round_of(k).wait_recv()
        hrow[...] = jnp.sum(hall[...], axis=0)
        for k in range(size):
            if k != 1:
                news(k).start()
        tot[...] = hrow[...]

    pl.when(jnp.logical_not(is_head))(news(0).wait_recv)
    sums = tot[...]
    pick = lambda k: jnp.broadcast_to(sums[:, k:k + 1], (1, 128))
    rz_all, curv_all, w_all = pick(0), pick(1), pick(2)
    alpha = rz_all / curv_all
    beta = alpha * (w_all / curv_all)
    for k in range(4):
        for half in range(2):
            at = pl.ds(128 * half, 128)
            zk = zt[k, :, at]
            sol_ref[k, :, at] = alpha * zk
            res_ref[k, :, at] = jnp.where(k < count, own[k, :, at], 0.0) - alpha * vt[k, :, at]
            dir_ref[k, :, at] = beta * zk - alpha * wt[k, :, at]

    for o in around:
        for copy in halo[o]:
            pl.when(there(*o))(copy.wait_send)
    pl.when(jnp.logical_not(is_head))(to_head.wait_send)
    pl.when(y > 0)(to_south.wait_send)
    pl.when((place == 0) & (px > 0))(to_back.wait_send)
    pl.when(s < ns - 1)(along[0].wait_send)
    pl.when(s > 0)(along[1].wait_send)
    pl.when(y > 0)(across[0].wait_send)
    pl.when(y < ny - 1)(across[1].wait_send)

    @pl.when(is_head)
    def _():
        for k in range(len(plane_set)):
            round_of(k).wait_send()
        for k in range(size):
            if k != 1:
                news(k).wait_send()


def flush(*refs):
    sources, targets, sem = refs[:3], refs[3:6], refs[6]
    copies = [pltpu.make_async_copy(a, b, sem.at[k]) for k, (a, b) in enumerate(zip(sources, targets))]
    for copy in copies:
        copy.start()
    for copy in copies:
        copy.wait()


def solution(mesh):
    ns, ny = mesh.shape["sfc"], mesh.shape["grp"]
    nx, nz, nc = SHAPES[ns]
    size, n_plane = nz * nc, nx * ny - 1
    dma = pltpu.SemaphoreType.DMA
    block = jax.ShapeDtypeStruct((4, E, 16 * E), F32)
    vmem = pl.BlockSpec(memory_space=pltpu.VMEM)
    hbm = pl.BlockSpec(memory_space=pltpu.HBM)
    slots = lambda k: pltpu.VMEM((k, E, 256), F32)
    fine = pltpu.VMEM((ROWS, 128), F32)
    coarse = pltpu.VMEM((COARSE, 128), F32)
    line = lambda *k: pltpu.VMEM((*k, 128), F32)

    def shards(source, layer_counts):
        parts = pl.pallas_call(
            functools.partial(kernel, (nx, nz, nc, ny)),
            out_shape=(block, block, block),
            in_specs=[hbm, hbm],
            out_specs=(vmem, vmem, vmem),
            scratch_shapes=[
                slots(4), pltpu.SMEM((1,), jnp.int32), pltpu.VMEM((E, 256), F32),
                slots(4), slots(4), slots(3), slots(3), *[fine] * 11,
                *[coarse] * 4, coarse, line(80), coarse, line(2, 64), line(2, 64), slots(4), slots(4), slots(4),
                line(8), line(4), line(1), line(8 * size), line(4 * size), line(1), line(n_plane + 1, 1),
                line(1), line(1),
                dma((2,)), dma((10,)), dma((10,)), dma((4,)), dma((4,)), dma((3,)), dma((size,)), dma((size,)),
                dma, dma((n_plane,)), dma((n_plane,)), dma((size,)), dma,
            ],
            compiler_params=pltpu.CompilerParams(
                collective_id=0, has_side_effects=True, vmem_limit_bytes=16 << 20),
        )(pltpu.with_memory_space_constraint(source, pltpu.HBM), layer_counts)
        return pl.pallas_call(
            flush, out_shape=(block, block, block), in_specs=[vmem] * 3, out_specs=(hbm,) * 3,
            scratch_shapes=[dma((3,))],
            compiler_params=pltpu.CompilerParams(vmem_limit_bytes=1 << 20),
        )(*parts)

    spec = P("sfc", None, "grp")
    return jax.shard_map(
        shards, mesh=mesh, in_specs=(spec, P("sfc")), out_specs=(spec, spec, spec), check_vma=False)
```

time: 53.2 us -> 38.8 us (0.73)
  Pallas kernels: 46 us -> 37.4 us
  between operations: 4.02 us -> 1.28 us
  other arithmetic: 1.62 us -> 0 us
  local copies, waits for them, and re-layouts: 1.21 us -> 0 us
    pallas_call x1, Pallas kernels: 46 us -> 36.7 us  [shards(): pl.pallas_call(functools.partial(kernel, (nx, nz, nc, ny)), out_shape=(bl...]
    mul x1 -> x0, other arithmetic: 1.61 us -> none  [shards(): return (alpha * z0, rhs - alpha * image, alpha * (wv / curv * z0 - w))]
    pallas_call x0 -> x1, Pallas kernels: none -> 0.7 us  [shards(): pl.pallas_call(flush, out_shape=(block, block, block), in_specs=[vmem] *...]
    unnamed x4 -> x0, local copies, waits for them, and re-layouts: 0.62 us -> none
    slice x1 -> x0, local copies, waits for them, and re-layouts: 0.59 us -> none  [shards(): rz, curv, wv = (total[0, 0], total[0, 1], total[0, 2])]
where the time goes in v2:
time: 38.8 us; the launch traced here: 38.7 us
  Pallas kernels  37.4 us (96%)
  between operations  1.28 us (3%)
    pallas_call x1, Pallas kernels, shards(): pl.pallas_call(functools.partial(kernel, (nx, nz, nc, ny)), out_shape=(bl...  36.7 us

profile of v2, /device:TPU:1, one launch (start us, length us, event | category | flops | bytes accessed | tf_op | source)
XLA Modules:
  0.0 38.7 jit_solution(3735146487388838848)
XLA Ops:
  1.3 36.7 %shard_map.49 = (f32[4,16,256]{2,1,0:T(8,128)S(1)}, f32[4,16,256]{2,1,0:T(8,128)S(1)}, f32[4,16,256]{2,1,0:T(8,128)S(1)}) custom-call(f32[4,16,256]{2,1,0:T(8,128)} %src_hbm.1, s32[1]{0:T(128)S(6)} %copy.5.cnt_hbm), custom_call_target="tpu_custom_call" | custom-call | tf_op jit(solution)/shard_map/pallas_call | solution.py:480
  38.0 0.7 %shard_map.50 = (f32[4,16,256]{2,1,0:T(8,128)}, f32[4,16,256]{2,1,0:T(8,128)}, f32[4,16,256]{2,1,0:T(8,128)}) custom-call(f32[4,16,256]{2,1,0:T(8,128)S(1)} %get-tuple-element.6.refs_0_, f32[4,16,256]{2,1,0:T(8,128)S(1)} %get-tuple-element.7.refs_1_, f32[4,16,256]{2,1,0:T(8,128)S(1)} %get-tuple-element.8.refs_2_), custom_call_target="tpu_custom_call" | custom-call | tf_op jit(solution)/shard_map/pallas_call | solution.py:497

commit v3 on v2

v3 whole, which is shorter than its diff:
```python
import functools

import jax
import jax.numpy as jnp
from jax import lax
from jax.experimental import pallas as pl
from jax.experimental.pallas import tpu as pltpu
from jax.sharding import PartitionSpec as P

E = 16
OMEGA = 2.0 / 3.0
STEP = OMEGA / 6.0
KEEP = 1.0 - OMEGA
TAU = OMEGA / 1.5
QUARTER = TAU / 4.0
SHAPES = {96: (4, 12, 2), 8: (2, 2, 2)}
MESH = pl.DeviceIdType.MESH
F32 = jnp.float32
FINE = 8 + 24 * 25
COARSE = 8 + 16 * 13
NEED = dict(g=1, q=2, c=1, e1=2, e2=3, e3=4, zp=8, z1=10, z0=11, v=12, g2=13, q2=14, c2=7)


def others(*axes):
    found = [()]
    for count in axes:
        found = [f + (i,) for f in found for i in range(count)]
    far = lambda f: -sum(min(i, n - i) for i, n in zip(f, axes))
    return sorted([f for f in found if any(f)], key=far)


def fine_row(j):
    return 8 + 24 * j


def coarse_row(j):
    return 8 + 16 * j


def kernel(dims, src_hbm, cnt_ref, sol_ref, res_ref, dir_ref, *scratch):
    nx, nz, nc, ny = dims
    (own, last, ysl, ynl, below, above, r, g, q, zp, z1, z0, v, g2, q2, w,
     c, e1, e2, e3, c2, kap, cd, cu, ca, cs, cn, zt, vt, wt,
     msg, face, faces, hb, hs, hx, hall, hrow, tot,
     load_sem, s1, r1, s2, r2, sm, rb, rs, rx, sh, rh, st, rt) = scratch
    s = lax.axis_index("sfc")
    y = lax.axis_index("grp")
    ns, size = nx * nz * nc, nz * nc
    px, place = s // size, lax.rem(s, size)
    is_head = place == 1
    plane_set = others(nx, ny)
    n_plane = len(plane_set)

    loads = [pltpu.make_async_copy(src_hbm.at[:, :, pl.ds(128 * h, 128)], own.at[h], load_sem.at[h]) for h in range(2)]
    for load in loads:
        load.start()

    around = [(1, 1), (1, -1), (-1, 1), (-1, -1), (1, 0), (-1, 0), (0, 1), (0, -1)]
    d_ok = {1: s < ns - 1, -1: s > 0, 0: None}
    y_ok = {1: y < ny - 1, -1: y > 0, 0: None}

    def there(ds, dy):
        conds = [k for k in (d_ok[ds], y_ok[dy]) if k is not None]
        return functools.reduce(jnp.logical_and, conds)

    def near(ds, dy):
        return (s + ds, y + dy)

    def head_of(x, yy):
        return (x * size + 1, yy)

    def plane(dx, dy):
        return (lax.rem(px + dx, nx) * size + 1, lax.rem(y + dy, ny))

    barrier = pltpu.get_barrier_semaphore()

    def greet(target):
        pl.semaphore_signal(barrier, inc=1, device_id=target, device_id_type=MESH)

    for o in around:
        pl.when(there(*o))(functools.partial(greet, near(*o)))

    @pl.when(is_head)
    def _():
        for o in plane_set:
            greet(plane(*o))
        for k in range(size):
            if k != 1:
                greet((px * size + k, y))

        @pl.when(y < ny - 1)
        def _():
            for k in range(size):
                greet((px * size + k, y + 1))

        @pl.when(px < nx - 1)
        def _():
            greet(((px + 1) * size, y))

    one = lambda cond: jnp.where(cond, 1, 0)
    beside = (1 + one(s > 0) + one(s < ns - 1)) * (1 + one(y > 0) + one(y < ny - 1)) - 1
    heads = one(y > 0) + one((place == 0) & (px > 0)) + jnp.where(is_head, n_plane, 1)

    blank = jnp.zeros((8, 128), F32)
    for array in (r, g, zp, z1, z0, v, g2):
        for b in range(2):
            for j in range(-1, 25):
                array[b, pl.ds(fine_row(j) + 16, 8), :] = blank
    for array in (c, e1, e2, c2, kap):
        for j in range(-1, 13):
            array[pl.ds(coarse_row(j) + 8, 8), :] = blank
    kap[pl.ds(coarse_row(7), 8), :] = blank

    def clear(cond, box):
        @pl.when(cond)
        def _():
            box[...] = jnp.zeros(box.shape, F32)

    clear(s == 0, below)
    clear(s == ns - 1, above)
    clear(y == 0, ysl)
    clear(y == 0, below.at[0])
    clear(y == 0, above.at[0])
    clear(y == ny - 1, ynl)
    clear(y == ny - 1, below.at[2])
    clear(y == ny - 1, above.at[2])

    count = cnt_ref[...]
    for h in range(2):
        loads[h].wait()
        final = own[h, 0]
        for k in range(1, 4):
            final = jnp.where(count > k, own[h, k], final)
        last[h] = final
    pl.semaphore_wait(barrier, beside + heads)

    def copy_to(src, dst, ss, rs_, target):
        return pltpu.make_async_remote_copy(
            src_ref=src, dst_ref=dst, send_sem=ss, recv_sem=rs_, device_id=target, device_id_type=MESH)

    halo = {}
    made = 0
    for o in around:
        ds, dy = o
        halo[o] = []
        for part in range(2 if dy else 1):
            half = 1 - part if dy == 1 else part
            if ds:
                src, box = (last, below.at[1 - dy]) if ds == 1 else (own.at[:, 0], above.at[1 - dy])
                if dy:
                    src, box = src.at[half], box.at[half]
                if part:
                    src, box = (ref.at[pl.ds(8 if ds == 1 else 0, 8)] for ref in (src, box))
            else:
                src, box = own.at[half], (ysl if dy == 1 else ynl).at[half]
            halo[o].append(copy_to(src, box, s1.at[made], r1.at[made], near(*o)))
            made += 1
    for part in range(2):
        for o in around:
            if part < len(halo[o]):
                pl.when(there(*o))(halo[o][part].start)

    def arrived(ds, dy, part=0):
        pl.when(there(-ds, -dy))(halo[ds, dy][part].wait_recv)

    lane = lax.broadcasted_iota(jnp.int32, (8, 128), 1)
    upper = lane >= 64
    pair = lax.rem(lane, 64)
    cnt8 = count[:8]
    end = 8 + 8 * cnt8
    alive = (pair >= 8) & (pair < end)
    lo_lane = jnp.where(s > 0, 8, 0)
    hi_lane = jnp.where(s < ns - 1, 8, 0)
    there_mask = (pair >= 8 - lo_lane) & (pair < end + hi_lane)
    mask = jnp.where(there_mask, 1.0, 0.0).astype(F32)
    outer = jnp.where(upper, jnp.where(y < ny - 1, mask, 0.0), jnp.where(y > 0, mask, 0.0))
    fine_masks = [outer * STEP, outer * STEP, mask * STEP]
    coarse_masks = [outer * QUARTER, outer * QUARTER, mask * QUARTER]
    pieces = (ysl, own, ynl)

    def assemble(block):
        for b in range(2):
            stack = []
            for m in (block, 5 - block):
                take = lambda ref, *k: ref[(*k, pl.ds(b, 8, stride=2), slice(None))]
                up = take(above, m // 2, m % 2)
                stack.append(take(below, m // 2, m % 2))
                for k in range(4):
                    mine = take(pieces[m // 2], m % 2, k)
                    stack.append(jnp.where(cnt8 == k, up, mine) if k else mine)
                stack += [up, blank, blank]
            turned = jnp.concatenate(stack, axis=0).T
            for j in range(8):
                for h in range(2):
                    low, high = turned[16 * j + 8 * h:16 * j + 8 * h + 8], turned[16 * (7 - j) + 8 * h:16 * (7 - j) + 8 * h + 8]
                    value = jnp.where(upper, high, low) * fine_masks[block]
                    r[b, pl.ds(fine_row(8 * block + j) + 8 * h, 8), :] = value
                    if block == 2 and j == 7:
                        r[b, pl.ds(fine_row(24) + 8 * h, 8), :] = pltpu.roll(value, 64, 1)

    def total(ref, b, j, h):
        i = fine_row(j) + 8 * h
        load8 = lambda k: ref[b, pl.ds(k, 8), :]
        across = ref[1 - b, pl.ds(i, 8), :]
        turned = pltpu.roll(across, 127 if b else 1, 1)
        return load8(i), ((load8(i - 24) + load8(i + 24)) + (load8(i - 1) + load8(i + 1))) + (across + turned)

    def put(dst, b, j, h, value):
        dst[b, pl.ds(fine_row(j) + 8 * h, 8), :] = value
        if j == 23:
            dst[b, pl.ds(fine_row(24) + 8 * h, 8), :] = pltpu.roll(value, 64, 1)

    def smooth(src, dst, add=None):
        def row(j):
            for b in range(2):
                for h in range(2):
                    mid, six = total(src, b, j, h)
                    value = KEEP * mid + fine_masks[j // 8] * six
                    if add is not None:
                        value = value + add[b, pl.ds(fine_row(j) + 8 * h, 8), :]
                    put(dst, b, j, h, value)
        return row

    def apply(src, dst):
        def row(j):
            for b in range(2):
                for h in range(2):
                    mid, six = total(src, b, j, h)
                    put(dst, b, j, h, OMEGA * mid - fine_masks[j // 8] * six)
        return row

    def put_coarse(dst, j, value):
        dst[pl.ds(coarse_row(j), 8), :] = value
        if j == 11:
            dst[pl.ds(coarse_row(12), 8), :] = pltpu.roll(value, 64, 1)

    def restrict(src, dst):
        def row(j):
            eight = None
            for b in range(2):
                for k in range(4):
                    part = src[b, pl.ds(fine_row(2 * j + k // 2) + k % 2, 8, stride=2), :]
                    eight = part if eight is None else eight + part
            put_coarse(dst, j, (0.125 * TAU / STEP) * eight)
        return row

    def coarse_total(ref, j):
        i = coarse_row(j)
        load8 = lambda k: ref[pl.ds(k, 8), :]
        mid = load8(i)
        sides = pltpu.roll(mid, 1, 1) + pltpu.roll(mid, 127, 1)
        return mid, ((load8(i - 16) + load8(i + 16)) + (load8(i - 1) + load8(i + 1))) + sides

    def coarse_first(rhs, dst):
        def row(j):
            mid, six = coarse_total(rhs, j)
            put_coarse(dst, j, (1.0 + KEEP) * mid + coarse_masks[j // 4] * six)
        return row

    def coarse_sweep(rhs, src, dst):
        def row(j):
            mid, six = coarse_total(src, j)
            put_coarse(dst, j, (KEEP * mid + rhs[pl.ds(coarse_row(j), 8), :]) + coarse_masks[j // 4] * six)
        return row

    def corrected(rhs, first, coarse, dst):
        def row(j):
            add = coarse[pl.ds(coarse_row(j), 8), :]
            for b in range(2):
                for k in range(4):
                    fine_j = 2 * j + k // 2
                    at = pl.ds(fine_row(fine_j) + k % 2, 8, stride=2)
                    value = (rhs[b, at, :] + first[b, at, :]) + add
                    dst[b, at, :] = value
                    if fine_j == 23:
                        dst[b, pl.ds(fine_row(24) + k % 2, 8, stride=2), :] = pltpu.roll(value, 64, 1)
        return row

    def rows(fn, lo, hi):
        for j in reversed(range(lo, hi)):
            fn(j)

    shrink = lambda lo: lo + 1
    halve = lambda lo: -(-lo // 2)
    double = lambda lo: 2 * lo
    stages = [
        ("g", "r", shrink, smooth(r, g)), ("q", "g", shrink, smooth(g, q)),
        ("c", "q", halve, restrict(q, c)), ("e1", "c", shrink, coarse_first(c, e1)),
        ("e2", "e1", shrink, coarse_sweep(c, e1, e2)), ("e3", "e2", shrink, coarse_sweep(c, e2, e3)),
        ("zp", "e3", double, corrected(r, g, e3, zp)), ("z1", "zp", shrink, smooth(zp, z1, r)),
        ("z0", "z1", shrink, smooth(z1, z0, r)), ("v", "z0", shrink, apply(z0, v)),
        ("g2", "v", shrink, smooth(v, g2)), ("q2", "g2", shrink, smooth(g2, q2)),
        ("c2", "q2", halve, restrict(q2, c2)),
    ]
    coarse_names = ("c", "e1", "e2", "e3", "c2")
    done = {}

    def advance(lo):
        have = {"r": lo}
        for name, source, change, fn in stages:
            start = max(change(have[source]), NEED[name])
            stop = done.get(name, 12 if name in coarse_names else 24)
            if start >= stop:
                break
            have[name] = done[name] = start
            if name == "zp":
                rows(fn, start // 2, stop // 2)
            else:
                rows(fn, start, stop)

    arrived(1, 0)
    arrived(-1, 0)
    assemble(2)
    advance(16)
    for dy in (1, -1):
        for ds in (1, -1, 0):
            arrived(ds, dy, 0)
    assemble(1)
    advance(8)
    for dy in (1, -1):
        for ds in (1, -1, 0):
            arrived(ds, dy, 1)
    assemble(0)
    advance(0)

    rz = curv = fine = coarse = blank
    for j in range(16, 24):
        for b in range(2):
            for h in range(2):
                at = (b, pl.ds(fine_row(j) + 8 * h, 8))
                vy, gy, qy, zy = v[at], g2[at], q2[at], z0[at]
                rz = rz + r[at] * zy
                curv = curv + zy * vy
                fine = fine + (vy * ((vy + gy) + qy) + gy * qy)
    for j in range(8, 12):
        mid, six = coarse_total(c2, j)
        put_coarse(kap, j, jnp.where(alive, KEEP * mid + coarse_masks[2] * six, 0.0))
    for j in range(8, 12):
        k, six = coarse_total(kap, j)
        cc = c2[pl.ds(coarse_row(j), 8), :]
        coarse = coarse + (cc * (cc + k) + k * ((1.0 + KEEP) * k + QUARTER * six))
    column = lambda value: jnp.sum(jnp.where(alive, value, 0.0), axis=0, keepdims=True)
    inner = jnp.concatenate([kap[pl.ds(coarse_row(j), 8), :] for j in range(8, 12)], axis=0)
    turned = jnp.concatenate([inner] * 4, axis=0).T
    cnt1, lane1 = cnt8[:1], lane[:1]
    ends = []
    for h in (0, 64):
        tail = turned[h + 15:h + 16]
        for k in range(2, 5):
            tail = jnp.where(cnt1 == k, turned[h + 7 + 8 * k:h + 8 + 8 * k], tail)
        ends.append((turned[h + 8:h + 9], tail))
    d_face = jnp.where(lane1 < 64, jnp.where(lane1 < 32, ends[0][0], ends[1][0]),
                       jnp.where(lane1 < 96, ends[0][1], ends[1][1]))
    sides = kap[pl.ds(coarse_row(8), 8), :]
    swapped = pltpu.roll(sides, 64, 1)
    north_face = jnp.where(upper[:4], sides[:4], swapped[4:])
    south_face = jnp.where(upper[:4], swapped[:4], sides[4:])
    msg[...] = jnp.concatenate(
        [column(rz), column(curv), (1.0 / STEP) * column(fine) + (8.0 / TAU) * column(coarse), d_face, north_face],
        axis=0)
    face[...] = south_face
    faces[...] = d_face

    order = [0] + list(range(2, size)) + [1]
    box = jnp.where(place > 1, place - 1, 0)
    box = jnp.where(is_head, size - 1, box)
    to_head = copy_to(msg, hb.at[pl.ds(pl.multiple_of(8 * box, 8), 8)], sm.at[0], rb, head_of(px, y))
    to_south = copy_to(face, hs.at[pl.ds(pl.multiple_of(4 * box, 4), 4)], sm.at[1], rs, head_of(px, y - 1))
    to_back = copy_to(faces, hx, sm.at[2], rx, head_of(px - 1, y))
    pl.when(jnp.logical_not(is_head))(to_head.start)
    pl.when(y > 0)(to_south.start)
    pl.when((place == 0) & (px > 0))(to_back.start)

    mine = jnp.concatenate([c2[pl.ds(coarse_row(j), 8), :] for j in range(8, 12)], axis=0)
    four = lambda x: jnp.concatenate([x] * 4, axis=0)
    cnt32, alive32 = four(cnt8), four(alive)

    def shifted(value, sign):
        out = pltpu.roll(value, (8 * sign) % 128, 1)
        for k in range(2, 5):
            out = jnp.where(cnt32 == k, pltpu.roll(value, (8 * k * sign) % 128, 1), out)
        return out

    cd[0] = shifted(mine, -1)
    cu[0] = mine
    along = [copy_to(cd.at[0], cd.at[1], s2.at[0], r2.at[0], near(1, 0)),
             copy_to(cu.at[0], cu.at[1], s2.at[1], r2.at[1], near(-1, 0))]
    pl.when(s < ns - 1)(along[0].start)
    pl.when(s > 0)(along[1].start)

    pl.when(s > 0)(along[0].wait_recv)
    pl.when(s < ns - 1)(along[1].wait_recv)
    lo32 = four((pair >= 8 - lo_lane) & (pair < 8))
    hi32 = four((pair >= end) & (pair < end + hi_lane))
    ca[...] = jnp.where(alive32, mine, jnp.where(lo32, cd[1], jnp.where(hi32, shifted(cu[1], 1), 0.0)))
    across = [copy_to(ca, cn, s2.at[2], r2.at[2], near(0, -1)),
              copy_to(ca, cs, s2.at[3], r2.at[3], near(0, 1))]
    pl.when(y > 0)(across[0].start)
    pl.when(y < ny - 1)(across[1].start)

    lines = copy_to(hb.at[pl.ds(0, 8 * (size - 1))], hb.at[pl.ds(0, 8 * (size - 1))], sm.at[0], rb, head_of(px, y))
    beyond = copy_to(hs, hs, sm.at[1], rs, head_of(px, y))
    rounds = copy_to(hall.at[pl.ds(0, n_plane)], hall.at[pl.ds(0, n_plane)], sh, rh, head_of(px, y))

    def round_of(k):
        return copy_to(hall.at[n_plane], hall.at[k], sh, rh, plane(*plane_set[k]))

    @pl.when(is_head)
    def _():
        hb[pl.ds(8 * (size - 1), 8), :] = msg[...]
        lines.wait_recv()
        pl.when(y < ny - 1)(beyond.wait_recv)
        pl.when(px < nx - 1)(to_back.wait_recv)
        acc = hb[pl.ds(0, 8), :]
        for k in range(1, size):
            acc = acc + hb[pl.ds(8 * k, 8), :]
        cross = jnp.zeros((4, 128), F32)
        for k in range(size):
            cross = cross + hb[pl.ds(8 * k + 4, 4), :] * hs[pl.ds(4 * k, 4), :]
        cross = jnp.where(y < ny - 1, jnp.sum(cross, axis=0, keepdims=True), 0.0)
        where_is = {p: k for k, p in enumerate(order)}
        front = hb[pl.ds(3, size, stride=8), :]
        back = pltpu.roll(front, 64, 1)
        row_of = lambda value, p: value[where_is[p]:where_is[p] + 1]
        chain = jnp.where(px < nx - 1, row_of(back, size - 1) * hx[...], 0.0)
        chain = chain + row_of(back, 0) * row_of(front, 1) + row_of(back, 1) * row_of(front, 2)
        run = back[1:size - 2] * hb[pl.ds(19, size - 3, stride=8), :]
        chain = chain + jnp.sum(run, axis=0, keepdims=True)
        cross = cross + jnp.where(lane1 < 64, chain, 0.0)
        three = jnp.concatenate([acc[:2], acc[2:3] + 4.0 * cross], axis=0)
        sums = jnp.sum(three, axis=1, keepdims=True)
        hall[n_plane] = jnp.where(lane1 == 0, sums[:1], jnp.where(lane1 == 1, sums[1:2], sums[2:]))
        for k in range(n_plane):
            round_of(k).start()

    def turn_back(src, dst):
        for b in range(2):
            stack = []
            for j in range(8):
                for h in range(2):
                    low, high = src[b, pl.ds(fine_row(16 + j) + 8 * h, 8), :], src[b, pl.ds(fine_row(23 - j) + 8 * h, 8), :]
                    stack.append(jnp.where(alive, jnp.where(upper, high, low), 0.0))
            x = jnp.concatenate(stack, axis=0).T
            for h in range(2):
                for k in range(4):
                    at = 64 * h + 8 * (k + 1)
                    dst[h, k, pl.ds(b, 8, stride=2), :] = x[at:at + 8]

    turn_back(z0, zt)
    turn_back(v, vt)

    pl.when(y > 0)(across[1].wait_recv)
    pl.when(y < ny - 1)(across[0].wait_recv)
    for j in range(4, 12):
        if j < 8:
            at = pl.ds(8 * (7 - j), 8)
            south = jnp.where(y > 0, pltpu.roll(cs[at, :], 64, 1), 0.0)
            north = jnp.where(y < ny - 1, pltpu.roll(cn[at, :], 64, 1), 0.0)
            put_coarse(c, j, jnp.where(upper, north, south))
        else:
            put_coarse(c, j, ca[pl.ds(8 * (j - 8), 8), :])
    rows(coarse_first(c, e1), 5, 12)
    rows(coarse_sweep(c, e1, e2), 6, 12)
    rows(coarse_sweep(c, e2, e3), 7, 12)
    rows(corrected(v, g2, e3, zp), 7, 12)
    rows(smooth(zp, z1, v), 15, 24)
    rows(smooth(z1, w, v), 16, 24)
    turn_back(w, wt)

    def news(k):
        return copy_to(hrow, tot, st, rt, (px * size + k, y))

    @pl.when(is_head)
    def _():
        rounds.wait_recv()
        hrow[...] = jnp.sum(hall[...], axis=0)
        for k in range(size):
            if k != 1:
                news(k).start()
        tot[...] = hrow[...]

    pl.when(jnp.logical_not(is_head))(news(0).wait_recv)
    sums = tot[...]
    pick = lambda k: jnp.broadcast_to(sums[:, k:k + 1], (1, 128))
    rz_all, curv_all, w_all = pick(0), pick(1), pick(2)
    alpha = rz_all / curv_all
    beta = alpha * (w_all / (curv_all * (1.0 / STEP)))
    scaled = alpha * (1.0 / STEP)
    for k in range(4):
        for half in range(2):
            at = pl.ds(128 * half, 128)
            zk = zt[half, k]
            sol_ref[k, :, at] = alpha * zk
            res_ref[k, :, at] = jnp.where(count > k, own[half, k], 0.0) - scaled * vt[half, k]
            dir_ref[k, :, at] = beta * zk - alpha * wt[half, k]

    for o in around:
        for copy in halo[o]:
            pl.when(there(*o))(copy.wait_send)
    pl.when(jnp.logical_not(is_head))(to_head.wait_send)
    pl.when(y > 0)(to_south.wait_send)
    pl.when((place == 0) & (px > 0))(to_back.wait_send)
    pl.when(s < ns - 1)(along[0].wait_send)
    pl.when(s > 0)(along[1].wait_send)
    pl.when(y > 0)(across[0].wait_send)
    pl.when(y < ny - 1)(across[1].wait_send)
    told = copy_to(hall.at[pl.ds(0, size - 1)], hall.at[pl.ds(0, size - 1)], st, rt, head_of(px, y))

    @pl.when(is_head)
    def _():
        rounds.wait_send()
        told.wait_send()


def flush(*refs):
    sources, targets, sem = refs[:3], refs[3:6], refs[6]
    copies = [pltpu.make_async_copy(a, b, sem.at[k]) for k, (a, b) in enumerate(zip(sources, targets))]
    for copy in copies:
        copy.start()
    for copy in copies:
        copy.wait()


def solution(mesh):
    ns, ny = mesh.shape["sfc"], mesh.shape["grp"]
    nx, nz, nc = SHAPES[ns]
    size, n_plane = nz * nc, nx * ny - 1
    dma = pltpu.SemaphoreType.DMA
    block = jax.ShapeDtypeStruct((4, E, 16 * E), F32)
    vmem = pl.BlockSpec(memory_space=pltpu.VMEM)
    hbm = pl.BlockSpec(memory_space=pltpu.HBM)
    slots = lambda *k: pltpu.VMEM((*k, E, 128), F32)
    fine = pltpu.VMEM((2, FINE, 128), F32)
    coarse = pltpu.VMEM((COARSE, 128), F32)
    line = lambda *k: pltpu.VMEM((*k, 128), F32)

    def shards(source, layer_counts):
        counts = jnp.broadcast_to(layer_counts.reshape(1, 1), (16, 128))
        parts = pl.pallas_call(
            functools.partial(kernel, (nx, nz, nc, ny)),
            out_shape=(block, block, block),
            in_specs=[hbm, vmem],
            out_specs=(vmem, vmem, vmem),
            scratch_shapes=[
                slots(2, 4), slots(2), slots(2, 4), slots(2, 4), slots(3, 2), slots(3, 2), *[fine] * 10,
                *[coarse] * 6, line(2, 32), line(2, 32), line(32), line(32), line(32),
                slots(2, 4), slots(2, 4), slots(2, 4),
                line(8), line(4), line(1), line(8 * size), line(4 * size), line(1), line(n_plane + 1, 1),
                line(1), line(1),
                dma((2,)), dma((14,)), dma((14,)), dma((4,)), dma((4,)), dma((3,)), dma, dma,
                dma, dma, dma, dma, dma,
            ],
            compiler_params=pltpu.CompilerParams(
                collective_id=0, has_side_effects=True, vmem_limit_bytes=24 << 20),
        )(pltpu.with_memory_space_constraint(source, pltpu.HBM), counts)
        return pl.pallas_call(
            flush, out_shape=(block, block, block), in_specs=[vmem] * 3, out_specs=(hbm,) * 3,
            scratch_shapes=[dma((3,))],
            compiler_params=pltpu.CompilerParams(vmem_limit_bytes=1 << 20),
        )(*parts)

    spec = P("sfc", None, "grp")
    return jax.shard_map(
        shards, mesh=mesh, in_specs=(spec, P("sfc")), out_specs=(spec, spec, spec), check_vma=False)
```

time: 38.8 us -> 37.1 us (0.956)
  Pallas kernels: 37.4 us -> 35.6 us
    pallas_call x1, Pallas kernels: 36.7 us -> 34.9 us  [shards(): pl.pallas_call(functools.partial(kernel, (nx, nz, nc, ny)), out_shape=(bl...]
where the time goes in v3:
time: 37.1 us; the launch traced here: 36.9 us
  Pallas kernels  35.6 us (96%)
  between operations  1.29 us (3%)
    pallas_call x1, Pallas kernels, shards(): pl.pallas_call(functools.partial(kernel, (nx, nz, nc, ny)), out_shape=(bl...  34.9 us

profile of v3, /device:TPU:1, one launch (start us, length us, event | category | flops | bytes accessed | tf_op | source)
XLA Modules:
  0.0 36.9 jit_solution(15832531134124171450)
XLA Ops:
  1.3 34.9 %shard_map.49 = (f32[4,16,256]{2,1,0:T(8,128)S(1)}, f32[4,16,256]{2,1,0:T(8,128)S(1)}, f32[4,16,256]{2,1,0:T(8,128)S(1)}) custom-call(f32[4,16,256]{2,1,0:T(8,128)} %src_hbm.1, s32[16,128]{1,0:T(8,128)S(1)} %broadcast_in_dim.8.cnt_ref), custom_call_target="tpu_custom_call" | custom-call | tf_op jit(solution)/shard_map/pallas_call | solution.py:539
  36.2 0.7 %shard_map.50 = (f32[4,16,256]{2,1,0:T(8,128)}, f32[4,16,256]{2,1,0:T(8,128)}, f32[4,16,256]{2,1,0:T(8,128)}) custom-call(f32[4,16,256]{2,1,0:T(8,128)S(1)} %get-tuple-element.6.refs_0_, f32[4,16,256]{2,1,0:T(8,128)S(1)} %get-tuple-element.7.refs_1_, f32[4,16,256]{2,1,0:T(8,128)S(1)} %get-tuple-element.8.refs_2_), custom_call_target="tpu_custom_call" | custom-call | tf_op jit(solution)/shard_map/pallas_call | solution.py:556
  (1 shorter events, 0.0 us)

commit v4 on v3

--- a/solution.py
+++ b/solution.py
@@ -37,12 +37,12 @@
     return 8 + 16 * j
 
 
-def kernel(dims, src_hbm, cnt_ref, sol_ref, res_ref, dir_ref, *scratch):
+def body(dims, src_hbm, cnt_ref, sol_ref, res_ref, dir_ref, scratch, s1, s2, sm, sh, st, load_sem):
     nx, nz, nc, ny = dims
     (own, last, ysl, ynl, below, above, r, g, q, zp, z1, z0, v, g2, q2, w,
      c, e1, e2, e3, c2, kap, cd, cu, ca, cs, cn, zt, vt, wt,
      msg, face, faces, hb, hs, hx, hall, hrow, tot,
-     load_sem, s1, r1, s2, r2, sm, rb, rs, rx, sh, rh, st, rt) = scratch
+     r1, r2, rb, rs, rx, rh, rt) = scratch
     s = lax.axis_index("sfc")
     y = lax.axis_index("grp")
     ns, size = nx * nz * nc, nz * nc
@@ -467,19 +467,31 @@
     rows(smooth(z1, w, v), 16, 24)
     turn_back(w, wt)
 
-    def news(k):
-        return copy_to(hrow, tot, st, rt, (px * size + k, y))
+    def news(k, yy):
+        return copy_to(hrow, tot, st, rt, (px * size + k, yy))
+
+    is_first = is_head & (px == 0) & (y == 0)
+    tells = is_head & jnp.logical_not(is_first)
+    tells_two = is_head & (px == 0) & (y == 1)
 
     @pl.when(is_head)
     def _():
         rounds.wait_recv()
-        hrow[...] = jnp.sum(hall[...], axis=0)
-        for k in range(size):
-            if k != 1:
-                news(k).start()
-        tot[...] = hrow[...]
-
-    pl.when(jnp.logical_not(is_head))(news(0).wait_recv)
+        total_row = jnp.sum(hall[...], axis=0)
+        hrow[...] = total_row
+        tot[...] = total_row
+
+    @pl.when(tells_two)
+    def _():
+        for k in list(range(2, size)) + [0]:
+            news(k, 0).start()
+
+    @pl.when(tells)
+    def _():
+        for k in [0] + list(range(2, size)):
+            news(k, y).start()
+
+    pl.when(jnp.logical_not(is_head))(news(0, y).wait_recv)
     sums = tot[...]
     pick = lambda k: jnp.broadcast_to(sums[:, k:k + 1], (1, 128))
     rz_all, curv_all, w_all = pick(0), pick(1), pick(2)
@@ -506,10 +518,16 @@
     pl.when(y < ny - 1)(across[1].wait_send)
     told = copy_to(hall.at[pl.ds(0, size - 1)], hall.at[pl.ds(0, size - 1)], st, rt, head_of(px, y))
 
-    @pl.when(is_head)
-    def _():
-        rounds.wait_send()
-        told.wait_send()
+    pl.when(is_head)(rounds.wait_send)
+    pl.when(tells)(told.wait_send)
+    pl.when(tells_two)(told.wait_send)
+
+
+def kernel(dims, src_hbm, cnt_ref, sol_ref, res_ref, dir_ref, *scratch):
+    dma = pltpu.SemaphoreType.DMA
+    pl.run_scoped(
+        functools.partial(body, dims, src_hbm, cnt_ref, sol_ref, res_ref, dir_ref, scratch),
+        dma((14,)), dma((4,)), dma((3,)), dma, dma, dma((2,)))
 
 
 def flush(*refs):
@@ -547,8 +565,7 @@
                 slots(2, 4), slots(2, 4), slots(2, 4),
                 line(8), line(4), line(1), line(8 * size), line(4 * size), line(1), line(n_plane + 1, 1),
                 line(1), line(1),
-                dma((2,)), dma((14,)), dma((14,)), dma((4,)), dma((4,)), dma((3,)), dma, dma,
-                dma, dma, dma, dma, dma,
+                dma((14,)), dma((4,)), dma, dma, dma, dma, dma,
             ],
             compiler_params=pltpu.CompilerParams(
                 collective_id=0, has_side_effects=True, vmem_limit_bytes=24 << 20),

time: 37.1 us -> 36.1 us (0.973)
  Pallas kernels: 35.6 us -> 34.6 us
    pallas_call x1, Pallas kernels: 34.9 us -> 33.9 us  [shards(): pl.pallas_call(functools.partial(kernel, (nx, nz, nc, ny)), out_shape=(bl...]
where the time goes in v4:
time: 36.1 us; the launch traced here: 35.9 us
  Pallas kernels  34.6 us (96%)
  between operations  1.29 us (4%)
    pallas_call x1, Pallas kernels, shards(): pl.pallas_call(functools.partial(kernel, (nx, nz, nc, ny)), out_shape=(bl...  33.9 us

profile of v4, /device:TPU:1, one launch (start us, length us, event | category | flops | bytes accessed | tf_op | source)
XLA Modules:
  0.0 35.9 jit_solution(9330452423065403646)
XLA Ops:
  1.3 33.9 %shard_map.49 = (f32[4,16,256]{2,1,0:T(8,128)S(1)}, f32[4,16,256]{2,1,0:T(8,128)S(1)}, f32[4,16,256]{2,1,0:T(8,128)S(1)}) custom-call(f32[4,16,256]{2,1,0:T(8,128)} %src_hbm.1, s32[16,128]{1,0:T(8,128)S(1)} %broadcast_in_dim.8.cnt_ref), custom_call_target="tpu_custom_call" | custom-call | tf_op jit(solution)/shard_map/pallas_call | solution.py:557
  35.2 0.7 %shard_map.50 = (f32[4,16,256]{2,1,0:T(8,128)}, f32[4,16,256]{2,1,0:T(8,128)}, f32[4,16,256]{2,1,0:T(8,128)}) custom-call(f32[4,16,256]{2,1,0:T(8,128)S(1)} %get-tuple-element.6.refs_0_, f32[4,16,256]{2,1,0:T(8,128)S(1)} %get-tuple-element.7.refs_1_, f32[4,16,256]{2,1,0:T(8,128)S(1)} %get-tuple-element.8.refs_2_), custom_call_target="tpu_custom_call" | custom-call | tf_op jit(solution)/shard_map/pallas_call | solution.py:573
  (1 shorter events, 0.0 us)

commit v5 on v4

--- a/solution.py
+++ b/solution.py
@@ -27,6 +27,12 @@
         found = [f + (i,) for f in found for i in range(count)]
     far = lambda f: -sum(min(i, n - i) for i, n in zip(f, axes))
     return sorted([f for f in found if any(f)], key=far)
+
+
+def tree(values):
+    while len(values) > 1:
+        values = [a + b for a, b in zip(values[::2], values[1::2])] + values[len(values) // 2 * 2:]
+    return values[0]
 
 
 def fine_row(j):
@@ -295,9 +301,11 @@
     coarse_names = ("c", "e1", "e2", "e3", "c2")
     done = {}
 
-    def advance(lo):
+    def advance(lo, until=None):
         have = {"r": lo}
         for name, source, change, fn in stages:
+            if name == until:
+                break
             start = max(change(have[source]), NEED[name])
             stop = done.get(name, 12 if name in coarse_names else 24)
             if start >= stop:
@@ -316,7 +324,7 @@
         for ds in (1, -1, 0):
             arrived(ds, dy, 0)
     assemble(1)
-    advance(8)
+    advance(8, 'g2')
     for dy in (1, -1):
         for ds in (1, -1, 0):
             arrived(ds, dy, 1)
@@ -349,8 +357,10 @@
         for k in range(2, 5):
             tail = jnp.where(cnt1 == k, turned[h + 7 + 8 * k:h + 8 + 8 * k], tail)
         ends.append((turned[h + 8:h + 9], tail))
-    d_face = jnp.where(lane1 < 64, jnp.where(lane1 < 32, ends[0][0], ends[1][0]),
-                       jnp.where(lane1 < 96, ends[0][1], ends[1][1]))
+    second = lax.rem(lane1, 64) >= 32
+    first_face, last_face = (jnp.where(second, ends[1][k], ends[0][k]) for k in range(2))
+    swap = jnp.where(lax.rem(place, 2) == 1, 64, 0)
+    d_face = jnp.where((lane1 >= swap) & (lane1 < swap + 64), first_face, last_face)
     sides = kap[pl.ds(coarse_row(8), 8), :]
     swapped = pltpu.roll(sides, 64, 1)
     north_face = jnp.where(upper[:4], sides[:4], swapped[4:])
@@ -411,22 +421,16 @@
         lines.wait_recv()
         pl.when(y < ny - 1)(beyond.wait_recv)
         pl.when(px < nx - 1)(to_back.wait_recv)
-        acc = hb[pl.ds(0, 8), :]
-        for k in range(1, size):
-            acc = acc + hb[pl.ds(8 * k, 8), :]
-        cross = jnp.zeros((4, 128), F32)
-        for k in range(size):
-            cross = cross + hb[pl.ds(8 * k + 4, 4), :] * hs[pl.ds(4 * k, 4), :]
+        acc = tree([hb[pl.ds(8 * k, 8), :] for k in range(size)])
+        cross = tree([hb[pl.ds(8 * k + 4, 4), :] * hs[pl.ds(4 * k, 4), :] for k in range(size)])
         cross = jnp.where(y < ny - 1, jnp.sum(cross, axis=0, keepdims=True), 0.0)
         where_is = {p: k for k, p in enumerate(order)}
-        front = hb[pl.ds(3, size, stride=8), :]
-        back = pltpu.roll(front, 64, 1)
-        row_of = lambda value, p: value[where_is[p]:where_is[p] + 1]
-        chain = jnp.where(px < nx - 1, row_of(back, size - 1) * hx[...], 0.0)
-        chain = chain + row_of(back, 0) * row_of(front, 1) + row_of(back, 1) * row_of(front, 2)
-        run = back[1:size - 2] * hb[pl.ds(19, size - 3, stride=8), :]
-        chain = chain + jnp.sum(run, axis=0, keepdims=True)
-        cross = cross + jnp.where(lane1 < 64, chain, 0.0)
+        row_at = lambda p: hb[pl.ds(8 * where_is[p] + 3, 1), :]
+        pairs = [[], []]
+        for p in range(size - 1):
+            pairs[p % 2].append(row_at(p) * row_at(p + 1))
+        pairs[1].append(jnp.where(px < nx - 1, row_at(size - 1) * hx[...], 0.0))
+        cross = cross + jnp.where(lane1 < 64, tree(pairs[1]), tree(pairs[0]))
         three = jnp.concatenate([acc[:2], acc[2:3] + 4.0 * cross], axis=0)
         sums = jnp.sum(three, axis=1, keepdims=True)
         hall[n_plane] = jnp.where(lane1 == 0, sums[:1], jnp.where(lane1 == 1, sums[1:2], sums[2:]))
@@ -477,7 +481,7 @@
     @pl.when(is_head)
     def _():
         rounds.wait_recv()
-        total_row = jnp.sum(hall[...], axis=0)
+        total_row = tree([hall[k] for k in range(n_plane + 1)])
         hrow[...] = total_row
         tot[...] = total_row
 

time: 36.1 us -> 36 us (level)
  no operation moved by 1% of the time
where the time goes in v5:
time: 36 us; the launch traced here: 35.8 us
  Pallas kernels  34.5 us (96%)
  between operations  1.29 us (4%)
    pallas_call x1, Pallas kernels, shards(): pl.pallas_call(functools.partial(kernel, (nx, nz, nc, ny)), out_shape=(bl...  33.8 us

profile of v5, /device:TPU:1, one launch (start us, length us, event | category | flops | bytes accessed | tf_op | source)
XLA Modules:
  0.0 35.8 jit_solution(6008010247606228455)
XLA Ops:
  1.3 33.8 %shard_map.49 = (f32[4,16,256]{2,1,0:T(8,128)S(1)}, f32[4,16,256]{2,1,0:T(8,128)S(1)}, f32[4,16,256]{2,1,0:T(8,128)S(1)}) custom-call(f32[4,16,256]{2,1,0:T(8,128)} %src_hbm.1, s32[16,128]{1,0:T(8,128)S(1)} %broadcast_in_dim.8.cnt_ref), custom_call_target="tpu_custom_call" | custom-call | tf_op jit(solution)/shard_map/pallas_call | solution.py:561
  35.1 0.7 %shard_map.50 = (f32[4,16,256]{2,1,0:T(8,128)}, f32[4,16,256]{2,1,0:T(8,128)}, f32[4,16,256]{2,1,0:T(8,128)}) custom-call(f32[4,16,256]{2,1,0:T(8,128)S(1)} %get-tuple-element.6.refs_0_, f32[4,16,256]{2,1,0:T(8,128)S(1)} %get-tuple-element.7.refs_1_, f32[4,16,256]{2,1,0:T(8,128)S(1)} %get-tuple-element.8.refs_2_), custom_call_target="tpu_custom_call" | custom-call | tf_op jit(solution)/shard_map/pallas_call | solution.py:577
  (1 shorter events, 0.0 us)

commit v6 on v5

--- a/solution.py
+++ b/solution.py
@@ -43,12 +43,12 @@
     return 8 + 16 * j
 
 
-def body(dims, src_hbm, cnt_ref, sol_ref, res_ref, dir_ref, scratch, s1, s2, sm, sh, st, load_sem):
+def body(dims, src_hbm, cnt_ref, sol_ref, res_ref, dir_ref, scratch,
+         s1, r1, s2, r2, sm, rb, rs, rx, sh, rh, st, rt, load_sem):
     nx, nz, nc, ny = dims
     (own, last, ysl, ynl, below, above, r, g, q, zp, z1, z0, v, g2, q2, w,
      c, e1, e2, e3, c2, kap, cd, cu, ca, cs, cn, zt, vt, wt,
-     msg, face, faces, hb, hs, hx, hall, hrow, tot,
-     r1, r2, rb, rs, rx, rh, rt) = scratch
+     msg, face, faces, hb, hs, hx, hall, hrow, tot) = scratch
     s = lax.axis_index("sfc")
     y = lax.axis_index("grp")
     ns, size = nx * nz * nc, nz * nc
@@ -69,8 +69,13 @@
         conds = [k for k in (d_ok[ds], y_ok[dy]) if k is not None]
         return functools.reduce(jnp.logical_and, conds)
 
+    def beside_of(k, step, count):
+        if step == 0:
+            return k
+        return jnp.where(k < count - 1, k + 1, 0) if step == 1 else jnp.where(k > 0, k - 1, count - 1)
+
     def near(ds, dy):
-        return (s + ds, y + dy)
+        return (beside_of(s, ds, ns), beside_of(y, dy, ny))
 
     def head_of(x, yy):
         return (x * size + 1, yy)
@@ -97,11 +102,11 @@
         @pl.when(y < ny - 1)
         def _():
             for k in range(size):
-                greet((px * size + k, y + 1))
+                greet((px * size + k, beside_of(y, 1, ny)))
 
         @pl.when(px < nx - 1)
         def _():
-            greet(((px + 1) * size, y))
+            greet((beside_of(px, 1, nx) * size, y))
 
     one = lambda cond: jnp.where(cond, 1, 0)
     beside = (1 + one(s > 0) + one(s < ns - 1)) * (1 + one(y > 0) + one(y < ny - 1)) - 1
@@ -375,8 +380,8 @@
     box = jnp.where(place > 1, place - 1, 0)
     box = jnp.where(is_head, size - 1, box)
     to_head = copy_to(msg, hb.at[pl.ds(pl.multiple_of(8 * box, 8), 8)], sm.at[0], rb, head_of(px, y))
-    to_south = copy_to(face, hs.at[pl.ds(pl.multiple_of(4 * box, 4), 4)], sm.at[1], rs, head_of(px, y - 1))
-    to_back = copy_to(faces, hx, sm.at[2], rx, head_of(px - 1, y))
+    to_south = copy_to(face, hs.at[pl.ds(pl.multiple_of(4 * box, 4), 4)], sm.at[1], rs, head_of(px, beside_of(y, -1, ny)))
+    to_back = copy_to(faces, hx, sm.at[2], rx, head_of(beside_of(px, -1, nx), y))
     pl.when(jnp.logical_not(is_head))(to_head.start)
     pl.when(y > 0)(to_south.start)
     pl.when((place == 0) & (px > 0))(to_back.start)
@@ -531,7 +536,7 @@
     dma = pltpu.SemaphoreType.DMA
     pl.run_scoped(
         functools.partial(body, dims, src_hbm, cnt_ref, sol_ref, res_ref, dir_ref, scratch),
-        dma((14,)), dma((4,)), dma((3,)), dma, dma, dma((2,)))
+        dma((14,)), dma((14,)), dma((4,)), dma((4,)), dma((3,)), *[dma] * 7, dma((2,)))
 
 
 def flush(*refs):
@@ -569,7 +574,6 @@
                 slots(2, 4), slots(2, 4), slots(2, 4),
                 line(8), line(4), line(1), line(8 * size), line(4 * size), line(1), line(n_plane + 1, 1),
                 line(1), line(1),
-                dma((14,)), dma((4,)), dma, dma, dma, dma, dma,
             ],
             compiler_params=pltpu.CompilerParams(
                 collective_id=0, has_side_effects=True, vmem_limit_bytes=24 << 20),

time: 36 us -> 35.8 us (level)
  no operation moved by 1% of the time
where the time goes in v6:
time: 35.8 us; the launch traced here: 35.5 us
  Pallas kernels  34.3 us (96%)
  between operations  1.29 us (4%)
    pallas_call x1, Pallas kernels, shards(): pl.pallas_call(functools.partial(kernel, (nx, nz, nc, ny)), out_shape=(bl...  33.6 us

profile of v6, /device:TPU:1, one launch (start us, length us, event | category | flops | bytes accessed | tf_op | source)
XLA Modules:
  0.0 35.5 jit_solution(18270398603181386380)
XLA Ops:
  1.3 33.6 %shard_map.49 = (f32[4,16,256]{2,1,0:T(8,128)S(1)}, f32[4,16,256]{2,1,0:T(8,128)S(1)}, f32[4,16,256]{2,1,0:T(8,128)S(1)}) custom-call(f32[4,16,256]{2,1,0:T(8,128)} %src_hbm.1, s32[16,128]{1,0:T(8,128)S(1)} %broadcast_in_dim.8.cnt_ref), custom_call_target="tpu_custom_call" | custom-call | tf_op jit(solution)/shard_map/pallas_call | solution.py:566
  34.8 0.7 %shard_map.50 = (f32[4,16,256]{2,1,0:T(8,128)}, f32[4,16,256]{2,1,0:T(8,128)}, f32[4,16,256]{2,1,0:T(8,128)}) custom-call(f32[4,16,256]{2,1,0:T(8,128)S(1)} %get-tuple-element.6.refs_0_, f32[4,16,256]{2,1,0:T(8,128)S(1)} %get-tuple-element.7.refs_1_, f32[4,16,256]{2,1,0:T(8,128)S(1)} %get-tuple-element.8.refs_2_), custom_call_target="tpu_custom_call" | custom-call | tf_op jit(solution)/shard_map/pallas_call | solution.py:581
  (1 shorter events, 0.0 us)

commit v7 on v6

--- a/solution.py
+++ b/solution.py
@@ -329,7 +329,7 @@
         for ds in (1, -1, 0):
             arrived(ds, dy, 0)
     assemble(1)
-    advance(8, 'g2')
+    advance(8, 'z0')
     for dy in (1, -1):
         for ds in (1, -1, 0):
             arrived(ds, dy, 1)
@@ -476,6 +476,18 @@
     rows(smooth(z1, w, v), 16, 24)
     turn_back(w, wt)
 
+    for o in around:
+        for copy in halo[o]:
+            pl.when(there(*o))(copy.wait_send)
+    pl.when(jnp.logical_not(is_head))(to_head.wait_send)
+    pl.when(y > 0)(to_south.wait_send)
+    pl.when((place == 0) & (px > 0))(to_back.wait_send)
+    pl.when(s < ns - 1)(along[0].wait_send)
+    pl.when(s > 0)(along[1].wait_send)
+    pl.when(y > 0)(across[0].wait_send)
+    pl.when(y < ny - 1)(across[1].wait_send)
+    pl.when(is_head)(rounds.wait_send)
+
     def news(k, yy):
         return copy_to(hrow, tot, st, rt, (px * size + k, yy))
 
@@ -515,19 +527,8 @@
             res_ref[k, :, at] = jnp.where(count > k, own[half, k], 0.0) - scaled * vt[half, k]
             dir_ref[k, :, at] = beta * zk - alpha * wt[half, k]
 
-    for o in around:
-        for copy in halo[o]:
-            pl.when(there(*o))(copy.wait_send)
-    pl.when(jnp.logical_not(is_head))(to_head.wait_send)
-    pl.when(y > 0)(to_south.wait_send)
-    pl.when((place == 0) & (px > 0))(to_back.wait_send)
-    pl.when(s < ns - 1)(along[0].wait_send)
-    pl.when(s > 0)(along[1].wait_send)
-    pl.when(y > 0)(across[0].wait_send)
-    pl.when(y < ny - 1)(across[1].wait_send)
     told = copy_to(hall.at[pl.ds(0, size - 1)], hall.at[pl.ds(0, size - 1)], st, rt, head_of(px, y))
 
-    pl.when(is_head)(rounds.wait_send)
     pl.when(tells)(told.wait_send)
     pl.when(tells_two)(told.wait_send)
 

time: 35.8 us -> 35.6 us (level)
  no operation moved by 1% of the time
where the time goes in v7:
time: 35.6 us; the launch traced here: 35.4 us
  Pallas kernels  34.1 us (96%)
  between operations  1.29 us (4%)
    pallas_call x1, Pallas kernels, shards(): pl.pallas_call(functools.partial(kernel, (nx, nz, nc, ny)), out_shape=(bl...  33.4 us

profile of v7, /device:TPU:1, one launch (start us, length us, event | category | flops | bytes accessed | tf_op | source)
XLA Modules:
  0.0 35.4 jit_solution(17725492328276141005)
XLA Ops:
  1.3 33.4 %shard_map.49 = (f32[4,16,256]{2,1,0:T(8,128)S(1)}, f32[4,16,256]{2,1,0:T(8,128)S(1)}, f32[4,16,256]{2,1,0:T(8,128)S(1)}) custom-call(f32[4,16,256]{2,1,0:T(8,128)} %src_hbm.1, s32[16,128]{1,0:T(8,128)S(1)} %broadcast_in_dim.8.cnt_ref), custom_call_target="tpu_custom_call" | custom-call | tf_op jit(solution)/shard_map/pallas_call | solution.py:567
  34.7 0.7 %shard_map.50 = (f32[4,16,256]{2,1,0:T(8,128)}, f32[4,16,256]{2,1,0:T(8,128)}, f32[4,16,256]{2,1,0:T(8,128)}) custom-call(f32[4,16,256]{2,1,0:T(8,128)S(1)} %get-tuple-element.6.refs_0_, f32[4,16,256]{2,1,0:T(8,128)S(1)} %get-tuple-element.7.refs_1_, f32[4,16,256]{2,1,0:T(8,128)S(1)} %get-tuple-element.8.refs_2_), custom_call_target="tpu_custom_call" | custom-call | tf_op jit(solution)/shard_map/pallas_call | solution.py:582
  (1 shorter events, 0.0 us)

commit v8 on v7

--- a/solution.py
+++ b/solution.py
@@ -88,7 +88,7 @@
     def greet(target):
         pl.semaphore_signal(barrier, inc=1, device_id=target, device_id_type=MESH)
 
-    for o in around:
+    for o in around[6:] + around[:6]:
         pl.when(there(*o))(functools.partial(greet, near(*o)))
 
     @pl.when(is_head)
@@ -166,10 +166,14 @@
                 src, box = own.at[half], (ysl if dy == 1 else ynl).at[half]
             halo[o].append(copy_to(src, box, s1.at[made], r1.at[made], near(*o)))
             made += 1
-    for part in range(2):
-        for o in around:
-            if part < len(halo[o]):
-                pl.when(there(*o))(halo[o][part].start)
+    for o, part in (
+            *[(o, 0) for o in around[4:6]],
+            *[(o, 0) for o in around[:4]],
+            *[(o, 1) for o in around[:4]],
+            *[(o, 0) for o in around[6:]],
+            *[(o, 1) for o in around[6:]],
+    ):
+        pl.when(there(*o))(halo[o][part].start)
 
     def arrived(ds, dy, part=0):
         pl.when(there(-ds, -dy))(halo[ds, dy][part].wait_recv)

time: 35.6 us -> 35.5 us (level)
  no operation moved by 1% of the time
where the time goes in v8:
time: 35.5 us; the launch traced here: 35.3 us
  Pallas kernels  34 us (96%)
  between operations  1.29 us (4%)
    pallas_call x1, Pallas kernels, shards(): pl.pallas_call(functools.partial(kernel, (nx, nz, nc, ny)), out_shape=(bl...  33.3 us

profile of v8, /device:TPU:1, one launch (start us, length us, event | category | flops | bytes accessed | tf_op | source)
XLA Modules:
  0.0 35.3 jit_solution(1144984782859985795)
XLA Ops:
  1.3 33.3 %shard_map.49 = (f32[4,16,256]{2,1,0:T(8,128)S(1)}, f32[4,16,256]{2,1,0:T(8,128)S(1)}, f32[4,16,256]{2,1,0:T(8,128)S(1)}) custom-call(f32[4,16,256]{2,1,0:T(8,128)} %src_hbm.1, s32[16,128]{1,0:T(8,128)S(1)} %broadcast_in_dim.8.cnt_ref), custom_call_target="tpu_custom_call" | custom-call | tf_op jit(solution)/shard_map/pallas_call | solution.py:571
  34.6 0.7 %shard_map.50 = (f32[4,16,256]{2,1,0:T(8,128)}, f32[4,16,256]{2,1,0:T(8,128)}, f32[4,16,256]{2,1,0:T(8,128)}) custom-call(f32[4,16,256]{2,1,0:T(8,128)S(1)} %get-tuple-element.6.refs_0_, f32[4,16,256]{2,1,0:T(8,128)S(1)} %get-tuple-element.7.refs_1_, f32[4,16,256]{2,1,0:T(8,128)S(1)} %get-tuple-element.8.refs_2_), custom_call_target="tpu_custom_call" | custom-call | tf_op jit(solution)/shard_map/pallas_call | solution.py:586
  (1 shorter events, 0.0 us)

commit v9 on v8

--- a/solution.py
+++ b/solution.py
@@ -25,8 +25,9 @@
     found = [()]
     for count in axes:
         found = [f + (i,) for f in found for i in range(count)]
-    far = lambda f: -sum(min(i, n - i) for i, n in zip(f, axes))
-    return sorted([f for f in found if any(f)], key=far)
+    late = [tuple(-i % n for i, n in zip(f, axes)) for f in found]
+    rank = {f: (-min(l[-1], axes[-1] - l[-1]), -l[0]) for f, l in zip(found, late)}
+    return sorted([f for f in found if any(f)], key=rank.get)
 
 
 def tree(values):

time: 35.5 us -> 35.5 us (level)
  no operation moved by 1% of the time
where the time goes in v9:
time: 35.5 us; the launch traced here: 35.3 us
  Pallas kernels  34 us (96%)
  between operations  1.29 us (4%)
    pallas_call x1, Pallas kernels, shards(): pl.pallas_call(functools.partial(kernel, (nx, nz, nc, ny)), out_shape=(bl...  33.3 us

profile of v9, /device:TPU:1, one launch (start us, length us, event | category | flops | bytes accessed | tf_op | source)
XLA Modules:
  0.0 35.3 jit_solution(14777120972061599975)
XLA Ops:
  1.3 33.3 %shard_map.49 = (f32[4,16,256]{2,1,0:T(8,128)S(1)}, f32[4,16,256]{2,1,0:T(8,128)S(1)}, f32[4,16,256]{2,1,0:T(8,128)S(1)}) custom-call(f32[4,16,256]{2,1,0:T(8,128)} %src_hbm.1, s32[16,128]{1,0:T(8,128)S(1)} %broadcast_in_dim.8.cnt_ref), custom_call_target="tpu_custom_call" | custom-call | tf_op jit(solution)/shard_map/pallas_call | solution.py:572
  34.6 0.7 %shard_map.50 = (f32[4,16,256]{2,1,0:T(8,128)}, f32[4,16,256]{2,1,0:T(8,128)}, f32[4,16,256]{2,1,0:T(8,128)}) custom-call(f32[4,16,256]{2,1,0:T(8,128)S(1)} %get-tuple-element.6.refs_0_, f32[4,16,256]{2,1,0:T(8,128)S(1)} %get-tuple-element.7.refs_1_, f32[4,16,256]{2,1,0:T(8,128)S(1)} %get-tuple-element.8.refs_2_), custom_call_target="tpu_custom_call" | custom-call | tf_op jit(solution)/shard_map/pallas_call | solution.py:587
  (1 shorter events, 0.0 us)
